TPU v7x, 256 devices: a whole 4x4x8 slice. The times are simulated.
256 devices in a mesh: row: 8 (over y, core), col: 32 (over x, z).
Axes of the slice: x: 4, y: 4, z: 8, core: 2. Of those that a mesh axis runs over, the one named last changes fastest.
Arguments:
- inner_base: bfloat16 [4, 1, 2, 4096, 14336], P(None, None, None, 'row', 'col'), may hold values from -250 to 250
- inner_left: bfloat16 [4, 1, 2, 4096, 16], P(None, None, None, ('row', 'col')), may hold values from -6 to 6
- inner_right: bfloat16 [4, 1, 2, 16, 14336], P(None, None, None, 'row', 'col'), may hold values from -12 to 12
- inner_mag: float32 [4, 1, 2, 14336], P(None, None, None, 'col'), may hold values from 512 to 2048
- outer_base: bfloat16 [4, 1, 14336, 4096], P(None, None, 'row', 'col'), may hold values from -250 to 250
- outer_left: bfloat16 [4, 1, 14336, 16], P(None, None, ('row', 'col')), may hold values from -6 to 6
- outer_right: bfloat16 [4, 1, 16, 4096], P(None, None, 'row', 'col'), may hold values from -12 to 12
- outer_mag: float32 [4, 1, 4096], P(None, None, 'col'), may hold values from 1792 to 7168
Outputs:
- inner_merged: bfloat16 [4, 1, 2, 4096, 14336], P(None, None, None, 'row', 'col')
- outer_merged: bfloat16 [4, 1, 14336, 4096], P(None, None, 'row', 'col')
All inputs are finite; a program needn't handle non-finite values.
Results may differ from a plain program's by a relative error of at most 0.001.
Values may be sent and summed in bfloat16 or wider, within the bound.
No kernel may reach another device: no remote copies, remote signals or barrier semaphores. Data moves between devices by JAX's collectives and lax.ppermute only.
A program may use at most 64 MiB of HBM per device.

v0:
```python
import jax
import jax.numpy as jnp
from jax import lax
from jax.sharding import PartitionSpec as P

epsilon = 1e-06


def from_everyone(value, axis):
    size = lax.axis_size(axis)
    return lax.all_to_all(
        jnp.broadcast_to(value[None], (size, *value.shape)), axis, 0, 0, tiled=True
    )


def over_copies(value, axis):
    return from_everyone(value, axis).sum(axis=0)


def packed_total(arrays, axis):
    line, at, finished = (jnp.concatenate([a.reshape(-1) for a in arrays]), 0, [])
    subtotal = over_copies(line, axis)
    for a in arrays:
        finished.append(subtotal[at : at + a.size].reshape(a.shape))
        at += a.size
    return tuple(finished)


def in_order(tiles, dim):
    lengths = list(tiles.shape[1:])
    lengths[dim] *= tiles.shape[0]
    return jnp.moveaxis(tiles, 0, dim).reshape(lengths)


def gathered_copies(value, axis, dim):
    tiles = from_everyone(value, axis)
    return in_order(tiles, dim)


def turned_gather(arrays, axis, dims):
    turned = [jnp.moveaxis(a, dim, 0) for a, dim in zip(arrays, dims)]
    both = jnp.concatenate([t.reshape(len(t), -1) for t in turned], axis=1)
    result, at, finished = (lax.all_gather(both, axis, axis=0, tiled=True), 0, [])
    for t, dim in zip(turned, dims):
        section = result[:, at : at + t[0].size].reshape(-1, *t.shape[1:])
        finished.append(jnp.moveaxis(section, 0, dim))
        at += t[0].size
    return tuple(finished)


def combine_tile(base, left, right):
    delta = jnp.einsum("...ik,...kj->...ij", left, right, preferred_element_type=jnp.float32)
    return base.astype(jnp.float32) + delta


def merge_layer(
    inner_base, outer_base, inner_mag, outer_mag, inner_left, outer_left, inner_right, outer_right
):
    inner_full = combine_tile(inner_base, inner_left, inner_right)
    outer_full = combine_tile(outer_base, outer_left, outer_right)
    inner_squares = jnp.sum(inner_full * inner_full, axis=-2)
    outer_squares = jnp.sum(outer_full * outer_full, axis=-2)
    inner_totals, outer_totals = packed_total((inner_squares, outer_squares), "row")
    inner_scale = lax.rsqrt(inner_totals + epsilon)
    outer_scale = lax.rsqrt(outer_totals + epsilon)
    inner_factor = inner_mag * inner_scale
    outer_factor = outer_mag * outer_scale
    inner_merged = (inner_factor[..., None, :] * inner_full).astype(jnp.bfloat16)
    outer_merged = (outer_factor[..., None, :] * outer_full).astype(jnp.bfloat16)
    return (inner_merged, outer_merged)


def shards(
    inner_base, inner_left, inner_right, inner_mag, outer_base, outer_left, outer_right, outer_mag
):
    layer_count = inner_base.shape[0]
    inner_outputs = []
    outer_outputs = []
    inner_rows, outer_rows = (
        gathered_copies(inner_left, "col", 3),
        gathered_copies(outer_left, "col", 2),
    )
    inner_ranks, outer_ranks = turned_gather((inner_right, outer_right), "row", (3, 2))
    for layer_index in range(layer_count):
        inner_merged, outer_merged = merge_layer(
            inner_base[layer_index],
            outer_base[layer_index],
            inner_mag[layer_index],
            outer_mag[layer_index],
            inner_rows[layer_index],
            outer_rows[layer_index],
            inner_ranks[layer_index],
            outer_ranks[layer_index],
        )
        inner_outputs.append(inner_merged)
        outer_outputs.append(outer_merged)
    return (jnp.stack(inner_outputs), jnp.stack(outer_outputs))


def solution(mesh):
    in_specs = (
        P(None, None, None, "row", "col"),
        P(None, None, None, ("row", "col"), None),
        P(None, None, None, "row", "col"),
        P(None, None, None, "col"),
        P(None, None, "row", "col"),
        P(None, None, ("row", "col"), None),
        P(None, None, "row", "col"),
        P(None, None, "col"),
    )
    out_specs = (P(None, None, None, "row", "col"), P(None, None, "row", "col"))
    return jax.shard_map(shards, mesh=mesh, in_specs=in_specs, out_specs=out_specs, check_vma=False)
```

profile of v0, /device:TPU:1, one launch (start us, length us, event | category | flops | bytes accessed | tf_op | source)
XLA Modules:
  0.0 110.4 jit_solution(7065436759786785537)
XLA Ops:
  0.7 0.9 copy.81
  1.7 1.8 %reshape.406 = bf16[32,2,1024]{2,1,0:T(2,128)(2,1)} reshape(bf16[32,4,1,2,16,16]{5,4,3,2,1,0:T(8,128)(2,1)S(1)} %broadcast_bitcast_fusion) | data formatting | bytes 262144
  3.5 11.9 %all-to-all-start = ((bf16[32,2,1024]{2,1,0:T(2,128)(2,1)}), bf16[32,2,1024]{2,1,0:T(2,128)(2,1)S(1)}, u32[]{:S(2)}, u32[]{:S(2)}) async-start(bf16[32,2,1024]{2,1,0:T(2,128)(2,1)} %reshape.406), calls=%async_computation | async-start | bytes 262144 | tf_op jit(solution)/shard_map/all_to_all | solution.py:11
  15.7 1.6 %fusion.20 = (bf16[1,1,1792,128]{3,2,1,0:T(8,128)(2,1)S(1)}, bf16[1,1,1792,128]{3,2,1,0:T(8,128)(2,1)S(1)}, bf16[1,1,1792,128]{3,2,1,0:T(8,128)(2,1)S(1)}, bf16[1,1,1792,128]{3,2,1,0:T(8,128)(2,1)S(1)}) fusion(bf16[4,1,1792,128]{3,2,1,0:T(8,128)(2,1)} %param.12), kind=kLoop, calls=%fused_computation.68 | loop fusion | bytes 3670016 | tf_op jit(solution)/shard_map/slice | solution.py:87
  17.3 14.1 %all-gather = bf16[8,2,4096]{2,1,0:T(2,128)(2,1)S(1)} all-gather(bf16[1,2,4096]{2,1,0:T(2,128)(2,1)S(1)} %maximum_bitcast_fusion), channel_id=1, replica_groups=mesh['row'=8,'col'=32] {'row'}, dimensions={0}, use_global_device_ids=true | all-gather | bytes 147456 | tf_op jit(solution)/shard_map/all_gather | solution.py:43
  31.7 1.7 %reshape.408 = bf16[32,2,1792]{2,1,0:T(2,128)(2,1)} reshape(bf16[32,4,1,16,56]{4,3,2,1,0:T(8,128)(2,1)S(1)} %broadcast_bitcast_fusion.1) | data formatting | bytes 458752
  33.3 1.0 copy.107
  34.3 1.0 copy.109
  35.3 1.0 copy.108
  36.6 9.5 %all-to-all-start.1 = ((bf16[32,2,1792]{2,1,0:T(2,128)(2,1)}), bf16[32,2,1792]{2,1,0:T(2,128)(2,1)S(1)}, u32[]{:S(2)}, u32[]{:S(2)}) async-start(bf16[32,2,1792]{2,1,0:T(2,128)(2,1)} %reshape.408), calls=%async_computation.1 | async-start | bytes 458752 | tf_op jit(solution)/shard_map/all_to_all | solution.py:11
  46.1 0.7 reshape.407
  48.8 2.9 %multiply_reduce_fusion.2 = (f32[2,448]{1,0:T(2,128)S(1)}, f32[2,512,448]{1,2,0:T(8,128)}) fusion(bf16[2,512,16]{1,2,0:T(8,128)(2,1)S(1)} %reshape.382, bf16[4,1,2,16,448]{4,3,2,1,0:T(8,128)(2,1)S(1)} %bitcast.187, bf16[4,1,2,512,448]{3,4,2,1,0:T(8,128)(2,1)} %param.8), kind=kOutput, calls=%fused_computation.19 | convolution fusion | flops 16514176 | bytes 2821632 | tf_op jit(solution)/shard_map/...ik,...kj->...ij/dot_general | solution.py:52
  51.8 2.9 %multiply_reduce_fusion.1 = (f32[2,448]{1,0:T(2,128)S(1)}, f32[2,512,448]{1,2,0:T(8,128)}) fusion(bf16[2,512,16]{1,2,0:T(8,128)(2,1)S(1)} %reshape.387, bf16[4,1,2,16,448]{4,3,2,1,0:T(8,128)(2,1)S(1)} %bitcast.188, bf16[4,1,2,512,448]{3,4,2,1,0:T(8,128)(2,1)} %param.8), kind=kOutput, calls=%fused_computation.17 | convolution fusion | flops 16514176 | bytes 2821632 | tf_op jit(solution)/shard_map/...ik,...kj->...ij/dot_general | solution.py:52
  54.8 2.9 %multiply_reduce_fusion = (f32[2,448]{1,0:T(2,128)S(1)}, f32[2,512,448]{1,2,0:T(8,128)}) fusion(bf16[2,512,16]{1,2,0:T(8,128)(2,1)S(1)} %reshape.392, bf16[4,1,2,16,448]{4,3,2,1,0:T(8,128)(2,1)S(1)} %bitcast.189, bf16[4,1,2,512,448]{3,4,2,1,0:T(8,128)(2,1)} %param.8), kind=kOutput, calls=%fused_computation.15 | convolution fusion | flops 16514176 | bytes 2821632 | tf_op jit(solution)/shard_map/...ik,...kj->...ij/dot_general | solution.py:52
  57.7 2.9 %multiply_reduce_fusion.3 = (f32[2,448]{1,0:T(2,128)S(1)}, f32[2,512,448]{1,2,0:T(8,128)}) fusion(bf16[2,512,16]{1,2,0:T(8,128)(2,1)S(1)} %reshape.376, bf16[4,1,2,16,448]{4,3,2,1,0:T(8,128)(2,1)S(1)} %bitcast.190, bf16[4,1,2,512,448]{3,4,2,1,0:T(8,128)(2,1)} %param.8), kind=kOutput, calls=%fused_computation.21 | convolution fusion | flops 16514176 | bytes 2821632 | tf_op jit(solution)/shard_map/...ik,...kj->...ij/dot_general | solution.py:52
  60.7 0.9 reshape.409
  63.1 0.6 broadcast_in_dim.20
  63.7 4.2 %all-to-all-start.2 = ((f32[8,1,1024]{2,1,0:T(1,128)}), f32[8,1,1024]{2,1,0:T(1,128)S(1)}, u32[]{:S(2)}, u32[]{:S(2)}) async-start(f32[8,1,1024]{2,1,0:T(1,128)} %broadcast_in_dim.20), calls=%async_computation.2 | async-start | bytes 65536 | tf_op jit(solution)/shard_map/all_to_all | solution.py:11
  68.3 1.4 %multiply_reduce_fusion.6 = (f32[128]{0:T(128)S(1)}, f32[1792,128]{0,1:T(8,128)S(1)}) fusion(bf16[1792,16]{0,1:T(8,128)(2,1)S(1)} %reshape.385, bf16[1,1,16,128]{3,0,2,1:T(2,128)(2,1)S(1)} %get-tuple-element.35, bf16[1,1,1792,128]{2,3,1,0:T(8,128)(2,1)} %copy.108), kind=kOutput, calls=%fused_computation.32 | convolution fusion | flops 8257408 | bytes 1438208 | tf_op jit(solution)/shard_map/...ik,...kj->...ij/dot_general | solution.py:52
  69.7 1.2 %multiply_reduce_fusion.4 = (f32[128]{0:T(128)S(1)}, f32[1792,128]{0,1:T(8,128)}) fusion(bf16[1792,16]{0,1:T(8,128)(2,1)S(1)} %reshape.395, bf16[1,1,16,128]{3,0,2,1:T(2,128)(2,1)S(1)} %get-tuple-element.33, bf16[1,1,1792,128]{2,3,1,0:T(8,128)(2,1)S(1)} %copy.110), kind=kOutput, calls=%fused_computation.30 | convolution fusion | flops 8257408 | bytes 1438208 | tf_op jit(solution)/shard_map/...ik,...kj->...ij/dot_general | solution.py:52
  71.0 1.6 %all-to-all-done.2 = f32[8,1,1024]{2,1,0:T(1,128)S(1)} async-done(((f32[8,1,1024]{2,1,0:T(1,128)}), f32[8,1,1024]{2,1,0:T(1,128)S(1)}, u32[]{:S(2)}, u32[]{:S(2)}) %all-to-all-start.2) | async-done | bytes 32800 | tf_op jit(solution)/shard_map/all_to_all | solution.py:11
  72.6 0.6 broadcast_in_dim.22
  73.2 4.0 %all-to-all-start.4 = ((f32[8,1,1024]{2,1,0:T(1,128)}), f32[8,1,1024]{2,1,0:T(1,128)S(1)}, u32[]{:S(2)}, u32[]{:S(2)}) async-start(f32[8,1,1024]{2,1,0:T(1,128)} %broadcast_in_dim.22), calls=%async_computation.4 | async-start | bytes 65536 | tf_op jit(solution)/shard_map/all_to_all | solution.py:11
  77.2 4.7 %all-to-all-done.4 = f32[8,1,1024]{2,1,0:T(1,128)S(1)} async-done(((f32[8,1,1024]{2,1,0:T(1,128)}), f32[8,1,1024]{2,1,0:T(1,128)S(1)}, u32[]{:S(2)}, u32[]{:S(2)}) %all-to-all-start.4) | async-done | bytes 32800 | tf_op jit(solution)/shard_map/all_to_all | solution.py:11
  82.6 4.0 %all-to-all-start.3 = ((f32[8,1,1024]{2,1,0:T(1,128)}), f32[8,1,1024]{2,1,0:T(1,128)S(1)}, u32[]{:S(2)}, u32[]{:S(2)}) async-start(f32[8,1,1024]{2,1,0:T(1,128)} %broadcast_in_dim.21), calls=%async_computation.3 | async-start | bytes 65536 | tf_op jit(solution)/shard_map/all_to_all | solution.py:11
  86.6 4.7 %all-to-all-done.3 = f32[8,1,1024]{2,1,0:T(1,128)S(1)} async-done(((f32[8,1,1024]{2,1,0:T(1,128)}), f32[8,1,1024]{2,1,0:T(1,128)S(1)}, u32[]{:S(2)}, u32[]{:S(2)}) %all-to-all-start.3) | async-done | bytes 32800 | tf_op jit(solution)/shard_map/all_to_all | solution.py:11
  91.9 4.0 %all-to-all-start.5 = ((f32[8,1,1024]{2,1,0:T(1,128)}), f32[8,1,1024]{2,1,0:T(1,128)S(1)}, u32[]{:S(2)}, u32[]{:S(2)}) async-start(f32[8,1,1024]{2,1,0:T(1,128)} %broadcast_in_dim.23), calls=%async_computation.5 | async-start | bytes 65536 | tf_op jit(solution)/shard_map/all_to_all | solution.py:11
  96.1 4.5 %all-to-all-done.5 = f32[8,1,1024]{2,1,0:T(1,128)S(1)} async-done(((f32[8,1,1024]{2,1,0:T(1,128)}), f32[8,1,1024]{2,1,0:T(1,128)S(1)}, u32[]{:S(2)}, u32[]{:S(2)}) %all-to-all-start.5) | async-done | bytes 32800 | tf_op jit(solution)/shard_map/all_to_all | solution.py:11
  100.7 1.3 %fusion.10 = (bf16[1,1,1792,128]{2,3,1,0:T(8,128)(2,1)S(1)}, bf16[1,1,1792,128]{2,3,1,0:T(8,128)(2,1)S(1)}) fusion(f32[1792,128]{0,1:T(8,128)S(1)} %get-tuple-element.53, f32[128]{0:T(128)S(1)} %get-tuple-element.39, f32[1792,128]{0,1:T(8,128)} %get-tuple-element.49, f32[128]{0:T(128)S(1)} %get-tuple-element.38), kind=kLoop, calls=%fused_computation.36 | loop fusion | flops 917504 | bytes 2753536 | tf_op jit(solution)/shard_map/stack | solution.py:97
  102.5 2.3 %copy.98 = bf16[4,1,1792,128]{3,2,1,0:T(8,128)(2,1)} copy(bf16[4,1,1792,128]{2,3,1,0:T(8,128)(2,1)S(1)} %pad_maximum_fusion.1) | data formatting | bytes 3670016
  104.8 2.5 %fusion.6 = (bf16[1,1,2,512,448]{3,4,2,1,0:T(8,128)(2,1)S(1)}, bf16[1,1,2,512,448]{3,4,2,1,0:T(8,128)(2,1)S(1)}) fusion(f32[2,512,448]{1,2,0:T(8,128)} %get-tuple-element.55, f32[2,448]{1,0:T(2,128)S(1)} %get-tuple-element.31, f32[2,512,448]{1,2,0:T(8,128)} %get-tuple-element.51, f32[2,448]{1,0:T(2,128)S(1)} %get-tuple-element.30), kind=kLoop, calls=%fused_computation.24 | loop fusion | flops 1835008 | bytes 5512192 | tf_op jit(solution)/shard_map/stack | solution.py:97
  108.3 2.1 %pad_maximum_fusion = bf16[4,1,2,512,448]{3,4,2,1,0:T(8,128)(2,1)} fusion(bf16[1,1,2,512,448]{3,4,2,1,0:T(8,128)(2,1)S(1)} %get-tuple-element.59, bf16[1,1,2,512,448]{3,4,2,1,0:T(8,128)(2,1)S(1)} %get-tuple-element.58, bf16[1,1,2,512,448]{3,4,2,1,0:T(8,128)(2,1)S(1)} %get-tuple-element.57, bf16[1,1,2,512,448]{3,4,2,1,0:T(8,128)(2,1)S(1)} %get-tuple-element.56), kind=kLoop, calls=%fused_computation | loop fusion | flops 5505024 | bytes 7340032 | tf_op jit(solution)/shard_map/stack | solution.py:97
  (82 shorter events, 8.2 us)
Async XLA Ops:
  0.6 14.9 %copy-start = (bf16[4,1,56,16]{2,3,1,0:T(8,128)(2,1)S(1)}, bf16[4,1,56,16]{2,3,1,0:T(8,128)(2,1)}, u32[]{:S(2)}) copy-start(bf16[4,1,56,16]{2,3,1,0:T(8,128)(2,1)} %param.13) | copy-start | bytes 21508
  0.6 14.7 %copy-start.6 = (bf16[4,1,2,2,448]{4,3,2,1,0:T(2,128)(2,1)S(1)}, bf16[4,1,2,2,448]{4,3,2,1,0:T(2,128)(2,1)}, u32[]{:S(2)}) copy-start(bf16[4,1,2,2,448]{4,3,2,1,0:T(2,128)(2,1)} %param.10) | copy-start | bytes 43012
  3.5 33.0 %all-to-all-start = ((bf16[32,2,1024]{2,1,0:T(2,128)(2,1)}), bf16[32,2,1024]{2,1,0:T(2,128)(2,1)S(1)}, u32[]{:S(2)}, u32[]{:S(2)}) async-start(bf16[32,2,1024]{2,1,0:T(2,128)(2,1)} %reshape.406), calls=%async_computation | async-start | bytes 262144 | tf_op jit(solution)/shard_map/all_to_all | solution.py:11
  15.6 1.6 %copy-start.7 = (bf16[4,1,2,128]{3,2,1,0:T(2,128)(2,1)S(1)}, bf16[4,1,2,128]{3,2,1,0:T(2,128)(2,1)}, u32[]{:S(2)}) copy-start(bf16[4,1,2,128]{3,2,1,0:T(2,128)(2,1)} %param.14) | copy-start | bytes 6148
  36.6 24.1 %all-to-all-start.1 = ((bf16[32,2,1792]{2,1,0:T(2,128)(2,1)}), bf16[32,2,1792]{2,1,0:T(2,128)(2,1)S(1)}, u32[]{:S(2)}, u32[]{:S(2)}) async-start(bf16[32,2,1792]{2,1,0:T(2,128)(2,1)} %reshape.408), calls=%async_computation.1 | async-start | bytes 458752 | tf_op jit(solution)/shard_map/all_to_all | solution.py:11
  61.6 1.1 copy-start.4
  61.7 6.2 %copy-start.3 = (bf16[1,1,1792,128]{2,3,1,0:T(8,128)(2,1)S(1)}, bf16[1,1,1792,128]{2,3,1,0:T(8,128)(2,1)}, u32[]{:S(2)}) copy-start(bf16[1,1,1792,128]{2,3,1,0:T(8,128)(2,1)} %copy.109) | copy-start | bytes 1376260
  63.7 8.9 %all-to-all-start.2 = ((f32[8,1,1024]{2,1,0:T(1,128)}), f32[8,1,1024]{2,1,0:T(1,128)S(1)}, u32[]{:S(2)}, u32[]{:S(2)}) async-start(f32[8,1,1024]{2,1,0:T(1,128)} %broadcast_in_dim.20), calls=%async_computation.2 | async-start | bytes 65536 | tf_op jit(solution)/shard_map/all_to_all | solution.py:11
  68.3 32.3 %copy-start.8 = (f32[4,1,128]{2,1,0:T(1,128)S(1)}, f32[4,1,128]{2,1,0:T(1,128)}, u32[]{:S(2)}) copy-start(f32[4,1,128]{2,1,0:T(1,128)} %param.15) | copy-start | bytes 6148
  73.2 8.7 %all-to-all-start.4 = ((f32[8,1,1024]{2,1,0:T(1,128)}), f32[8,1,1024]{2,1,0:T(1,128)S(1)}, u32[]{:S(2)}, u32[]{:S(2)}) async-start(f32[8,1,1024]{2,1,0:T(1,128)} %broadcast_in_dim.22), calls=%async_computation.4 | async-start | bytes 65536 | tf_op jit(solution)/shard_map/all_to_all | solution.py:11
  82.6 8.7 %all-to-all-start.3 = ((f32[8,1,1024]{2,1,0:T(1,128)}), f32[8,1,1024]{2,1,0:T(1,128)S(1)}, u32[]{:S(2)}, u32[]{:S(2)}) async-start(f32[8,1,1024]{2,1,0:T(1,128)} %broadcast_in_dim.21), calls=%async_computation.3 | async-start | bytes 65536 | tf_op jit(solution)/shard_map/all_to_all | solution.py:11
  91.9 8.7 %all-to-all-start.5 = ((f32[8,1,1024]{2,1,0:T(1,128)}), f32[8,1,1024]{2,1,0:T(1,128)S(1)}, u32[]{:S(2)}, u32[]{:S(2)}) async-start(f32[8,1,1024]{2,1,0:T(1,128)} %broadcast_in_dim.23), calls=%async_computation.5 | async-start | bytes 65536 | tf_op jit(solution)/shard_map/all_to_all | solution.py:11
  102.5 2.3 %copy-start.5 = (f32[4,1,2,448]{3,2,1,0:T(2,128)S(1)}, f32[4,1,2,448]{3,2,1,0:T(2,128)}, u32[]{:S(2)}) copy-start(f32[4,1,2,448]{3,2,1,0:T(2,128)} %param.11) | copy-start | bytes 43012
  104.8 2.6 %copy-start.1 = (f32[2,512,448]{1,2,0:T(8,128)S(1)}, f32[2,512,448]{1,2,0:T(8,128)}, u32[]{:S(2)}) copy-start(f32[2,512,448]{1,2,0:T(8,128)} %get-tuple-element.47) | copy-start | bytes 5505028
  104.8 3.1 %copy-start.2 = (f32[2,512,448]{1,2,0:T(8,128)S(1)}, f32[2,512,448]{1,2,0:T(8,128)}, u32[]{:S(2)}) copy-start(f32[2,512,448]{1,2,0:T(8,128)} %get-tuple-element.43) | copy-start | bytes 5505028
where the time goes:
time: 111 us; the launch traced here: 110 us
  starting transfers between devices  37.4 us (34%)
  local copies, waits for them, and re-layouts  20.5 us (18%)
  waiting for transfers between devices  15.5 us (14%)
  matrix products  14.9 us (13%)
  blocking collectives  14.1 us (13%)
  other arithmetic  6.87 us (6%)
    all_to_all x6, starting transfers between devices, from_everyone(): lax.all_to_all(jnp.broadcast_to(value[None], (size, *value.shape)), axis,...  37.4 us
    all_to_all x6, waiting for transfers between devices, from_everyone(): lax.all_to_all(jnp.broadcast_to(value[None], (size, *value.shape)), axis,...  15.5 us
    dot_general x8, matrix products, combine_tile(): jnp.einsum('...ik,...kj->...ij', left, right, preferred_element_type=jnp....  14.9 us
    all_gather x1, blocking collectives, turned_gather(): lax.all_gather(both, axis, axis=0, tiled=True)  14.1 us
    unnamed x30, local copies, waits for them, and re-layouts  11.6 us
    another operation x6, other arithmetic, shards(): return (jnp.stack(inner_outputs), jnp.stack(outer_outputs))  6.63 us
    broadcast_in_dim x5, local copies, waits for them, and re-layouts, from_everyone(): jnp.broadcast_to(value[None], (size, *value.shape))  3.33 us
  transfers between devices with their start and end apart: 6, of which 4 were waited for; matrix products, arithmetic and copies ran while one was open for 23% of the time, Pallas kernels for 0%

commit v1 on v0

v1 whole, which is shorter than its diff:
```python
import jax
import jax.numpy as jnp
from jax import lax
from jax.experimental import pallas as pl
from jax.experimental.pallas import tpu as pltpu
from jax.sharding import PartitionSpec as P

epsilon = 1e-06
F32, BF16 = jnp.float32, jnp.bfloat16
MIB = 1 << 20


def iota(shape, dim):
    return lax.broadcasted_iota(jnp.int32, shape, dim)


def whole():
    return pl.BlockSpec(memory_space=pltpu.VMEM)


def params(mib):
    return pltpu.CompilerParams(vmem_limit_bytes=mib * MIB)


def dot(a, b, dims):
    return lax.dot_general(a, b, (dims, ((), ())), preferred_element_type=F32)


def pack_left_kernel(inner_ref, outer_ref, out_ref):
    k, lane = iota((16, 128), 0), iota((16, 128), 1)
    inner = jnp.zeros((16, 128), F32)
    for m in range(8):
        pick = (lane == 16 * (k // 2) + 2 * m + k % 2).astype(F32).astype(BF16)
        inner += dot(inner_ref[m], pick, ((1,), (0,)))
    k, lane = iota((16, 256), 0), iota((16, 256), 1)
    outer = jnp.zeros((56, 256), F32)
    for l in range(4):
        at = 8 * (k // 2) + 2 * l + k % 2
        pick = jnp.logical_or(lane == at, lane == at + 192).astype(F32).astype(BF16)
        outer += dot(outer_ref[l], pick, ((0,), (0,)))
    first = outer[0:32, 0:128]
    second = jnp.concatenate([outer[32:56, 128:256], jnp.zeros((8, 128), F32)], axis=0)
    block = jnp.concatenate([inner, first + second], axis=0).astype(BF16)
    for i in range(out_ref.shape[0]):
        out_ref[i] = block


def pack_right_kernel(inner_ref, outer_ref, out_ref):
    row, e = iota((16, 2), 0), iota((16, 2), 1)
    inner = jnp.zeros((16, 448), F32)
    for m in range(8):
        pick = (row == 2 * m + e).astype(F32).astype(BF16)
        inner += dot(pick, inner_ref[m], ((1,), (0,)))
    row, e = iota((8, 2), 0), iota((8, 2), 1)
    outer = jnp.zeros((8, 128), F32)
    for l in range(4):
        pick = (row == 2 * l + e).astype(F32).astype(BF16)
        outer += dot(pick, outer_ref[l], ((1,), (0,)))
    inner = jnp.concatenate([inner, jnp.zeros((16, 64), F32)], axis=1)
    outer = jnp.concatenate([outer, jnp.zeros((8, 384), F32)], axis=1)
    block = jnp.concatenate([inner, outer], axis=0).astype(BF16)
    for i in range(out_ref.shape[0]):
        out_ref[i] = block


def spread_right_kernel(right_ref, inner_ref, outer_ref):
    turned = right_ref[:, 0:16, :].reshape(128, 512).astype(F32).T[0:448, :]
    matrix = (iota((448, 128), 1) % 16) // 2
    for m in range(8):
        inner_ref[m] = jnp.where(matrix == m, turned, 0.0).astype(BF16)
    ranks = right_ref[:, 16:24, 0:128].astype(F32).reshape(64, 128)
    matrix = (iota((64, 128), 0) % 8) // 2
    zero = jnp.zeros((64, 128), F32)
    for l in range(4):
        one = jnp.where(matrix == l, ranks, 0.0)
        outer_ref[l, 0:64, :] = jnp.concatenate([one, zero], axis=1).astype(BF16)
        outer_ref[l, 64:128, :] = jnp.concatenate([zero, one], axis=1).astype(BF16)


def squares_kernel(
    left_ref, inner_right_ref, outer_right_ref, inner_ref, outer_ref, inner_full_ref, outer_full_ref, squares_ref
):
    left = left_ref[:, 0:16, :].reshape(512, 128)
    sums = []
    for m in range(8):
        full = inner_ref[m].astype(F32) + dot(inner_right_ref[m], left, ((1,), (1,)))
        inner_full_ref[m] = full
        square = full * full
        part = (square[:, 0:128] + square[:, 128:256]) + (square[:, 256:384] + square[:, 384:512])
        sums.append(jnp.sum(part.T, axis=0, keepdims=True))
    left = left_ref[:, 16:48, :].reshape(1024, 128)
    tails = []
    for l in range(4):
        delta = dot(left, outer_right_ref[l], ((1,), (0,)))
        total = jnp.zeros((8, 128), F32)
        for c in range(32):
            here = slice(56 * c, 56 * c + 56)
            two = jnp.concatenate([delta[32 * c : 32 * c + 32, 0:128], delta[32 * c : 32 * c + 24, 128:256]], axis=0)
            full = outer_ref[l, here, :].astype(F32) + two
            outer_full_ref[l, here, :] = full
            total += jnp.sum((full * full).reshape(7, 8, 128), axis=0)
        total = jnp.sum(total, axis=0, keepdims=True)
        tails += [total[:, 0:64], total[:, 64:128]]
    block = jnp.concatenate(
        [jnp.concatenate([s, t], axis=1) for s, t in zip(sums, tails)], axis=0
    )
    for i in range(squares_ref.shape[0]):
        squares_ref[i] = block


def scale_kernel(
    squares_ref, inner_mag_ref, outer_mag_ref, inner_full_ref, outer_full_ref, inner_out, outer_out, inner_buf, outer_buf, sems
):
    scale = lax.rsqrt(jnp.sum(squares_ref[...], axis=0) + epsilon)
    mags = jnp.concatenate([inner_mag_ref[i] for i in range(4)], axis=0)
    factor = (scale[:, 0:448] * mags).T
    copies = []
    for m in range(8):
        column = factor[:, m : m + 1]
        inner_buf[m] = (inner_full_ref[m] * column).astype(BF16)
        copies.append(pltpu.make_async_copy(inner_buf.at[m], inner_out.at[m], sems.at[m]))
        copies[-1].start()
        if m % 2:
            l = m // 2
            row = jnp.concatenate([scale[2 * l : 2 * l + 1, 448:512], scale[2 * l + 1 : 2 * l + 2, 448:512]], axis=1)
            row = row * outer_mag_ref[l]
            outer_buf[l] = (outer_full_ref[l] * row).astype(BF16)
            copies.append(pltpu.make_async_copy(outer_buf.at[l], outer_out.at[l], sems.at[8 + l]))
            copies[-1].start()
    for copy in copies:
        copy.wait()


def exchange(blocks, axis):
    return lax.all_to_all(blocks, axis, 0, 0, tiled=True)


def shards(
    inner_base, inner_left, inner_right, inner_mag, outer_base, outer_left, outer_right, outer_mag
):
    rows, cols = lax.axis_size("row"), lax.axis_size("col")
    inner_base = jnp.swapaxes(inner_base, 3, 4).reshape(8, 448, 512)
    outer_base = outer_base.reshape(4, 1792, 128)
    left = pl.pallas_call(
        pack_left_kernel,
        out_shape=pltpu.VMEM((cols, 48, 128), BF16),
        in_specs=[whole()] * 2,
        out_specs=whole(),
        compiler_params=params(4),
        name="pack_left",
    )(inner_left.reshape(8, 16, 16), jnp.swapaxes(outer_left, 2, 3).reshape(4, 16, 56))
    left = exchange(left, "col")
    right = pl.pallas_call(
        pack_right_kernel,
        out_shape=pltpu.VMEM((rows, 24, 512), BF16),
        in_specs=[whole()] * 2,
        out_specs=whole(),
        compiler_params=params(4),
        name="pack_right",
    )(inner_right.reshape(8, 2, 448), outer_right.reshape(4, 2, 128))
    right = exchange(right, "row")
    inner_ranks, outer_ranks = pl.pallas_call(
        spread_right_kernel,
        out_shape=(pltpu.VMEM((8, 448, 128), BF16), pltpu.VMEM((4, 128, 256), BF16)),
        in_specs=[whole()],
        out_specs=(whole(), whole()),
        compiler_params=params(4),
        name="spread_right",
    )(right)
    inner_full, outer_full, squares = pl.pallas_call(
        squares_kernel,
        out_shape=(
            pltpu.VMEM((8, 448, 512), F32),
            pltpu.VMEM((4, 1792, 128), F32),
            pltpu.VMEM((rows, 8, 512), F32),
        ),
        in_specs=[whole()] * 5,
        out_specs=(whole(),) * 3,
        compiler_params=params(12),
        name="squares",
    )(left, inner_ranks, outer_ranks, inner_base, outer_base)
    squares = exchange(squares, "row")
    inner_merged, outer_merged = pl.pallas_call(
        scale_kernel,
        out_shape=(
            jax.ShapeDtypeStruct((8, 448, 512), BF16),
            jax.ShapeDtypeStruct((4, 1792, 128), BF16),
        ),
        in_specs=[whole()] * 5,
        out_specs=(pl.BlockSpec(memory_space=pltpu.HBM),) * 2,
        scratch_shapes=[
            pltpu.VMEM((8, 448, 512), BF16),
            pltpu.VMEM((4, 1792, 128), BF16),
            pltpu.SemaphoreType.DMA((12,)),
        ],
        compiler_params=params(12),
        name="scale",
    )(squares, inner_mag.reshape(4, 2, 448), outer_mag, inner_full, outer_full)
    inner_merged = jnp.swapaxes(inner_merged.reshape(4, 1, 2, 448, 512), 3, 4)
    return inner_merged, outer_merged.reshape(4, 1, 1792, 128)


def solution(mesh):
    in_specs = (
        P(None, None, None, "row", "col"),
        P(None, None, None, ("row", "col"), None),
        P(None, None, None, "row", "col"),
        P(None, None, None, "col"),
        P(None, None, "row", "col"),
        P(None, None, ("row", "col"), None),
        P(None, None, "row", "col"),
        P(None, None, "col"),
    )
    out_specs = (P(None, None, None, "row", "col"), P(None, None, "row", "col"))
    return jax.shard_map(shards, mesh=mesh, in_specs=in_specs, out_specs=out_specs, check_vma=False)
```

time: 111 us -> 57.6 us (0.52)
  starting transfers between devices: 37.4 us -> 17 us
  matrix products: 14.9 us -> 0 us
  local copies, waits for them, and re-layouts: 20.5 us -> 6.41 us
  other arithmetic: 6.87 us -> 0 us
  Pallas kernels: 0 us -> 6.68 us
  blocking collectives: 14.1 us -> 12.1 us
  waiting for transfers between devices: 15.5 us -> 14.2 us
    all_to_all x6 -> x2, starting transfers between devices: 37.4 us -> 17 us  [exchange(): return lax.all_to_all(blocks, axis, 0, 0, tiled=True)]
    dot_general x8 -> x0, matrix products: 14.9 us -> none  [combine_tile(): jnp.einsum('...ik,...kj->...ij', left, right, preferred_element_type=jnp....]
    all_gather x1 -> x0, blocking collectives: 14.1 us -> none  [turned_gather(): lax.all_gather(both, axis, axis=0, tiled=True)]
    all_to_all x0 -> x1, blocking collectives: none -> 12.1 us  [exchange(): return lax.all_to_all(blocks, axis, 0, 0, tiled=True)]
    pallas_call x0 -> x5, Pallas kernels: none -> 6.68 us  [the longest x1 2.79 us: shards(): pl.pallas_call(scale_kernel, out_shape=(jax.ShapeDtypeStruct((8, 448, 512...]
    another operation x6 -> x0, other arithmetic: 6.63 us -> none  [shards(): return (jnp.stack(inner_outputs), jnp.stack(outer_outputs))]
    unnamed x30 -> x16, local copies, waits for them, and re-layouts: 11.6 us -> 6.41 us
    broadcast_in_dim x5 -> x0, local copies, waits for them, and re-layouts: 3.33 us -> none  [from_everyone(): jnp.broadcast_to(value[None], (size, *value.shape))]
  transfers between devices with their start and end apart: 6 -> 2, of which waited for: 4 -> 2; matrix products, arithmetic and copies ran while one was open for 23% -> 0% of each run, Pallas kernels for 0% -> 2%
where the time goes in v1:
time: 57.6 us; the launch traced here: 57 us
  starting transfers between devices  17 us (30%)
  waiting for transfers between devices  14.2 us (25%)
  blocking collectives  12.1 us (21%)
  Pallas kernels  6.68 us (12%)
  local copies, waits for them, and re-layouts  6.41 us (11%)
  between operations  0.67 us (1%)
    all_to_all x2, starting transfers between devices, exchange(): return lax.all_to_all(blocks, axis, 0, 0, tiled=True)  17 us
    all_to_all x2, waiting for transfers between devices, exchange(): return lax.all_to_all(blocks, axis, 0, 0, tiled=True)  14.2 us
    all_to_all x1, blocking collectives, exchange(): return lax.all_to_all(blocks, axis, 0, 0, tiled=True)  12.1 us
    unnamed x16, local copies, waits for them, and re-layouts  6.41 us
    pallas_call x1, Pallas kernels, shards(): pl.pallas_call(scale_kernel, out_shape=(jax.ShapeDtypeStruct((8, 448, 512...  2.79 us
    pallas_call x1, Pallas kernels, shards(): pl.pallas_call(squares_kernel, out_shape=(pltpu.VMEM((8, 448, 512), F32),...  1.81 us
  transfers between devices with their start and end apart: 2, of which 2 were waited for; matrix products, arithmetic and copies ran while one was open for 0% of the time, Pallas kernels for 2%

profile of v1, /device:TPU:1, one launch (start us, length us, event | category | flops | bytes accessed | tf_op | source)
XLA Modules:
  0.0 57.0 jit_solution(8479571711201071356)
XLA Ops:
  0.6 0.0 copy-start.5
  0.6 0.7 %copy-done.5 = bf16[4,1,2,2,448]{4,3,2,1,0:T(2,128)(2,1)S(1)} copy-done((bf16[4,1,2,2,448]{4,3,2,1,0:T(2,128)(2,1)S(1)}, bf16[4,1,2,2,448]{4,3,2,1,0:T(2,128)(2,1)}, u32[]{:S(2)}) %copy-start.5) | copy-done | bytes 14360
  1.3 0.0 copy-start.6
  1.4 0.7 %copy-done.6 = bf16[4,1,2,128]{3,2,1,0:T(2,128)(2,1)S(1)} copy-done((bf16[4,1,2,128]{3,2,1,0:T(2,128)(2,1)S(1)}, bf16[4,1,2,128]{3,2,1,0:T(2,128)(2,1)}, u32[]{:S(2)}) %copy-start.6) | copy-done | bytes 2072
  2.0 0.9 %pack_right.1 = bf16[8,24,512]{2,1,0:T(8,128)(2,1)} custom-call(bf16[8,2,448]{2,1,0:T(2,128)(2,1)S(1)} %bitcast.26, bf16[4,2,128]{2,1,0:T(2,128)(2,1)S(1)} %bitcast.27), custom_call_target="tpu_custom_call" | custom-call | tf_op jit(solution)/shard_map/pack_right/pallas_call | solution.py:153
  2.9 6.5 %all-to-all-start.1 = ((bf16[8,24,512]{2,1,0:T(8,128)(2,1)}), bf16[8,24,512]{2,1,0:T(8,128)(2,1)S(1)}, u32[]{:S(2)}, u32[]{:S(2)}) async-start(bf16[8,24,512]{2,1,0:T(8,128)(2,1)} %pack_right.1), calls=%async_computation.1 | async-start | bytes 393216 | tf_op jit(solution)/shard_map/all_to_all | solution.py:135
  9.4 0.0 copy-start.2
  9.4 0.8 %copy-done.2 = bf16[4,1,2,16,16]{4,3,2,1,0:T(8,128)(2,1)S(1)} copy-done((bf16[4,1,2,16,16]{4,3,2,1,0:T(8,128)(2,1)S(1)}, bf16[4,1,2,16,16]{4,3,2,1,0:T(8,128)(2,1)}, u32[]{:S(2)}) %copy-start.2) | copy-done | bytes 4120
  10.2 0.0 copy-start.4
  10.2 0.7 %copy-done.4 = bf16[4,1,56,16]{2,3,1,0:T(8,128)(2,1)S(1)} copy-done((bf16[4,1,56,16]{2,3,1,0:T(8,128)(2,1)S(1)}, bf16[4,1,56,16]{2,3,1,0:T(8,128)(2,1)}, u32[]{:S(2)}) %copy-start.4) | copy-done | bytes 7192
  10.9 1.0 %pack_left.1 = bf16[32,48,128]{2,1,0:T(8,128)(2,1)} custom-call(bf16[8,16,16]{2,1,0:T(8,128)(2,1)S(1)} %bitcast.23, bf16[4,16,56]{2,1,0:T(8,128)(2,1)S(1)} %bitcast.25), custom_call_target="tpu_custom_call" | custom-call | tf_op jit(solution)/shard_map/pack_left/pallas_call | solution.py:144
  11.9 3.4 %all-to-all-done.1.right_ref = bf16[8,24,512]{2,1,0:T(8,128)(2,1)S(1)} async-done(((bf16[8,24,512]{2,1,0:T(8,128)(2,1)}), bf16[8,24,512]{2,1,0:T(8,128)(2,1)S(1)}, u32[]{:S(2)}, u32[]{:S(2)}) %all-to-all-start.1) | async-done | bytes 196640 | tf_op jit(solution)/shard_map/all_to_all | solution.py:135
  15.3 10.5 %all-to-all-start = ((bf16[32,48,128]{2,1,0:T(8,128)(2,1)}), bf16[32,48,128]{2,1,0:T(8,128)(2,1)S(1)}, u32[]{:S(2)}, u32[]{:S(2)}) async-start(bf16[32,48,128]{2,1,0:T(8,128)(2,1)} %pack_left.1), calls=%async_computation | async-start | bytes 786432 | tf_op jit(solution)/shard_map/all_to_all | solution.py:135
  25.8 0.2 spread_right.1
  26.0 10.8 %all-to-all-done.left_ref = bf16[32,48,128]{2,1,0:T(8,128)(2,1)S(1)} async-done(((bf16[32,48,128]{2,1,0:T(8,128)(2,1)}), bf16[32,48,128]{2,1,0:T(8,128)(2,1)S(1)}, u32[]{:S(2)}, u32[]{:S(2)}) %all-to-all-start) | async-done | bytes 393248 | tf_op jit(solution)/shard_map/all_to_all | solution.py:135
  36.8 0.0 copy-start
  36.8 2.0 %copy-done = bf16[4,1,2,512,448]{3,4,2,1,0:T(8,128)(2,1)S(1)} copy-done((bf16[4,1,2,512,448]{3,4,2,1,0:T(8,128)(2,1)S(1)}, bf16[4,1,2,512,448]{3,4,2,1,0:T(8,128)(2,1)}, u32[]{:S(2)}) %copy-start) | copy-done | bytes 3670040
  38.8 0.0 copy-start.1
  38.8 1.5 %copy-done.1 = bf16[4,1,1792,128]{3,2,1,0:T(8,128)(2,1)S(1)} copy-done((bf16[4,1,1792,128]{3,2,1,0:T(8,128)(2,1)S(1)}, bf16[4,1,1792,128]{3,2,1,0:T(8,128)(2,1)}, u32[]{:S(2)}) %copy-start.1) | copy-done | bytes 1835032
  40.3 0.0 copy-start.3
  40.3 0.0 copy-start.7
  40.3 1.8 %squares.1 = (f32[8,448,512]{2,1,0:T(8,128)S(1)}, f32[4,1792,128]{2,1,0:T(8,128)S(1)}, f32[8,8,512]{2,1,0:T(8,128)S(1)}) custom-call(bf16[32,48,128]{2,1,0:T(8,128)(2,1)S(1)} %all-to-all-done.left_ref, bf16[8,448,128]{2,1,0:T(8,128)(2,1)S(1)} %get-tuple-element.9.inner_right_ref, bf16[4,128,256]{2,1,0:T(8,128)(2,1)S(1)} %get-tuple-element.10.outer_right_ref, ...), custom_call_target="tpu_custom_call" | custom-call | tf_op jit(solution)/shard_map/squares/pallas_call | solution.py:170
  42.1 12.1 %all_to_all.15.squares_ref = f32[8,8,512]{2,1,0:T(8,128)S(1)} all-to-all(f32[8,8,512]{2,1,0:T(8,128)S(1)} %get-tuple-element.11), channel_id=1, replica_groups=mesh['row'=8,'col'=32] {'row'}, dimensions={0} | all-to-all | bytes 262144 | tf_op jit(solution)/shard_map/all_to_all | solution.py:135
  54.2 0.0 copy-done.3
  54.2 0.0 copy-done.7
  54.2 2.8 %scale.1 = (bf16[8,448,512]{2,1,0:T(8,128)(2,1)}, bf16[4,1792,128]{2,1,0:T(8,128)(2,1)}) custom-call(f32[8,8,512]{2,1,0:T(8,128)S(1)} %all_to_all.15.squares_ref, f32[4,2,448]{2,1,0:T(2,128)S(1)} %bitcast.24, f32[4,1,128]{2,1,0:T(1,128)S(1)} %copy-done.7, f32[8,448,512]{2,1,0:T(8,128)S(1)} %get-tuple-element.12.inner_full_ref, ...), custom_call_target="tpu_custom_call" | custom-call | tf_op jit(solution)/shard_map/scale/pallas_call | solution.py:183
Async XLA Ops:
  0.6 0.7 %copy-start.5 = (bf16[4,1,2,2,448]{4,3,2,1,0:T(2,128)(2,1)S(1)}, bf16[4,1,2,2,448]{4,3,2,1,0:T(2,128)(2,1)}, u32[]{:S(2)}) copy-start(bf16[4,1,2,2,448]{4,3,2,1,0:T(2,128)(2,1)} %param.10) | copy-start | bytes 43012
  1.3 0.7 %copy-start.6 = (bf16[4,1,2,128]{3,2,1,0:T(2,128)(2,1)S(1)}, bf16[4,1,2,128]{3,2,1,0:T(2,128)(2,1)}, u32[]{:S(2)}) copy-start(bf16[4,1,2,128]{3,2,1,0:T(2,128)(2,1)} %param.14) | copy-start | bytes 6148
  2.9 12.4 %all-to-all-start.1 = ((bf16[8,24,512]{2,1,0:T(8,128)(2,1)}), bf16[8,24,512]{2,1,0:T(8,128)(2,1)S(1)}, u32[]{:S(2)}, u32[]{:S(2)}) async-start(bf16[8,24,512]{2,1,0:T(8,128)(2,1)} %pack_right.1), calls=%async_computation.1 | async-start | bytes 393216 | tf_op jit(solution)/shard_map/all_to_all | solution.py:135
  9.4 0.8 %copy-start.2 = (bf16[4,1,2,16,16]{4,3,2,1,0:T(8,128)(2,1)S(1)}, bf16[4,1,2,16,16]{4,3,2,1,0:T(8,128)(2,1)}, u32[]{:S(2)}) copy-start(bf16[4,1,2,16,16]{4,3,2,1,0:T(8,128)(2,1)} %param.9) | copy-start | bytes 12292
  10.2 0.7 %copy-start.4 = (bf16[4,1,56,16]{2,3,1,0:T(8,128)(2,1)S(1)}, bf16[4,1,56,16]{2,3,1,0:T(8,128)(2,1)}, u32[]{:S(2)}) copy-start(bf16[4,1,56,16]{2,3,1,0:T(8,128)(2,1)} %param.13) | copy-start | bytes 21508
  15.3 21.5 %all-to-all-start = ((bf16[32,48,128]{2,1,0:T(8,128)(2,1)}), bf16[32,48,128]{2,1,0:T(8,128)(2,1)S(1)}, u32[]{:S(2)}, u32[]{:S(2)}) async-start(bf16[32,48,128]{2,1,0:T(8,128)(2,1)} %pack_left.1), calls=%async_computation | async-start | bytes 786432 | tf_op jit(solution)/shard_map/all_to_all | solution.py:135
  36.8 2.0 %copy-start = (bf16[4,1,2,512,448]{3,4,2,1,0:T(8,128)(2,1)S(1)}, bf16[4,1,2,512,448]{3,4,2,1,0:T(8,128)(2,1)}, u32[]{:S(2)}) copy-start(bf16[4,1,2,512,448]{3,4,2,1,0:T(8,128)(2,1)} %param.8) | copy-start | bytes 11010052
  38.8 1.5 %copy-start.1 = (bf16[4,1,1792,128]{3,2,1,0:T(8,128)(2,1)S(1)}, bf16[4,1,1792,128]{3,2,1,0:T(8,128)(2,1)}, u32[]{:S(2)}) copy-start(bf16[4,1,1792,128]{3,2,1,0:T(8,128)(2,1)} %param.12) | copy-start | bytes 5505028
  40.3 13.9 %copy-start.3 = (f32[4,1,2,448]{3,2,1,0:T(2,128)S(1)}, f32[4,1,2,448]{3,2,1,0:T(2,128)}, u32[]{:S(2)}) copy-start(f32[4,1,2,448]{3,2,1,0:T(2,128)} %param.11) | copy-start | bytes 43012
  40.3 13.9 %copy-start.7 = (f32[4,1,128]{2,1,0:T(1,128)S(1)}, f32[4,1,128]{2,1,0:T(1,128)}, u32[]{:S(2)}) copy-start(f32[4,1,128]{2,1,0:T(1,128)} %outer_mag_ref.1) | copy-start | bytes 6148

commit v2 on v1

v2 whole, which is shorter than its diff:
```python
import jax
import jax.numpy as jnp
from jax import lax
from jax.experimental import pallas as pl
from jax.experimental.pallas import tpu as pltpu
from jax.sharding import PartitionSpec as P


epsilon = 1e-06
F32, BF16 = jnp.float32, jnp.bfloat16
MIB = 1 << 20
FAR = (3, 7, 5)
EARLY = 6


def iota(shape, dim):
    return lax.broadcasted_iota(jnp.int32, shape, dim)


def whole():
    return pl.BlockSpec(memory_space=pltpu.VMEM)


def in_hbm():
    return pl.BlockSpec(memory_space=pltpu.HBM)


def kept(value):
    return pltpu.with_memory_space_constraint(value, pltpu.HBM)


def params(mib):
    return pltpu.CompilerParams(vmem_limit_bytes=mib * MIB)


def fetch(pairs, sems):
    copies = [pltpu.make_async_copy(a, b, sems.at[i]) for i, (a, b) in enumerate(pairs)]
    for copy in copies:
        copy.start()
    for copy in copies:
        copy.wait()


def dot(a, b, dims):
    return lax.dot_general(a, b, (dims, ((), ())), preferred_element_type=F32)


def pack_kernel(
    inner_left_hbm, outer_left_hbm, inner_right_hbm, outer_right_hbm, left_out, right_out,
    inner_left_ref, outer_left_ref, inner_right_ref, outer_right_ref, sems
):
    fetch(
        [
            (inner_left_hbm, inner_left_ref),
            (outer_left_hbm, outer_left_ref),
            (inner_right_hbm, inner_right_ref),
            (outer_right_hbm, outer_right_ref),
        ],
        sems,
    )
    k, lane = iota((16, 128), 0), iota((16, 128), 1)
    inner = jnp.zeros((16, 128), F32)
    for m in range(8):
        pick = (lane == 16 * (k // 2) + 2 * m + k % 2).astype(F32).astype(BF16)
        inner += dot(inner_left_ref[m], pick, ((1,), (0,)))
    k, lane = iota((16, 256), 0), iota((16, 256), 1)
    outer = jnp.zeros((56, 256), F32)
    for l in range(4):
        at = 8 * (k // 2) + 2 * l + k % 2
        pick = jnp.logical_or(lane == at, lane == at + 192).astype(F32).astype(BF16)
        outer += dot(outer_left_ref[l], pick, ((0,), (0,)))
    first = outer[0:32, 0:128]
    second = jnp.concatenate([outer[32:56, 128:256], jnp.zeros((8, 128), F32)], axis=0)
    block = jnp.concatenate([inner, first + second], axis=0).astype(BF16)
    for i in range(left_out.shape[0]):
        left_out[i] = block
    row, e = iota((16, 2), 0), iota((16, 2), 1)
    inner = jnp.zeros((16, 448), F32)
    for m in range(8):
        pick = (row == 2 * m + e).astype(F32).astype(BF16)
        inner += dot(pick, inner_right_ref[m], ((1,), (0,)))
    row, e = iota((8, 2), 0), iota((8, 2), 1)
    outer = jnp.zeros((8, 128), F32)
    for l in range(4):
        pick = (row == 2 * l + e).astype(F32).astype(BF16)
        outer += dot(pick, outer_right_ref[l], ((1,), (0,)))
    inner = jnp.concatenate([inner, jnp.zeros((16, 64), F32)], axis=1)
    outer = jnp.concatenate([outer, jnp.zeros((8, 384), F32)], axis=1)
    right_out[...] = jnp.concatenate([inner, outer], axis=0).astype(BF16)


def gather_right_kernel(own_ref, one_ref, two_ref, three_ref, inner_ref, outer_ref, right_ref):
    me = lax.axis_index("row")
    for d, ref in zip((0, *FAR), (own_ref, one_ref, two_ref, three_ref)):
        for core in range(2):
            right_ref[me ^ (d ^ core)] = ref[core].astype(F32)
    inner_ref[...] = right_ref[:, 0:16, :].reshape(128, 512).T[0:448, :].astype(BF16)
    ranks = right_ref[:, 16:24, 0:128].reshape(64, 128)
    matrix = (iota((64, 128), 0) % 8) // 2
    zero = jnp.zeros((64, 128), F32)
    for l in range(4):
        one = jnp.where(matrix == l, ranks, 0.0)
        outer_ref[l, 0:64, :] = jnp.concatenate([one, zero], axis=1).astype(BF16)
        outer_ref[l, 64:128, :] = jnp.concatenate([zero, one], axis=1).astype(BF16)


def load_kernel(inner_hbm, inner_ref, sems):
    fetch([(inner_hbm.at[0:EARLY], inner_ref)], sems)


def squares_kernel(
    left_ref, inner_right_ref, outer_right_ref, early_ref, inner_hbm, outer_hbm,
    inner_full_ref, outer_full_ref, squares_ref, late_ref, outer_ref, sems
):
    def start_inner(i, carry):
        pltpu.make_async_copy(inner_hbm.at[EARLY + i], late_ref.at[i], sems.at[i]).start()
        return carry

    def start_outer(l, carry):
        pltpu.make_async_copy(outer_hbm.at[l], outer_ref.at[l], sems.at[8 - EARLY + l]).start()
        return carry

    lax.fori_loop(0, 8 - EARLY, start_inner, 0)
    lax.fori_loop(0, 4, start_outer, 0)
    left = left_ref[:, 0:16, :].reshape(512, 128)
    matrix = (iota((1, 128), 1) % 16) // 2
    sums = []
    for m in range(8):
        if m == EARLY:
            for i in range(8 - EARLY):
                pltpu.make_async_copy(inner_hbm.at[EARLY + i], late_ref.at[i], sems.at[i]).wait()
            for l in range(4):
                pltpu.make_async_copy(outer_hbm.at[l], outer_ref.at[l], sems.at[8 - EARLY + l]).wait()
        base = early_ref[m] if m < EARLY else late_ref[m - EARLY]
        right = inner_right_ref[...] * (matrix == m).astype(F32).astype(BF16)
        full = base.astype(F32) + dot(right, left, ((1,), (1,)))
        inner_full_ref[m] = full
        square = full * full
        part = (square[:, 0:128] + square[:, 128:256]) + (square[:, 256:384] + square[:, 384:512])
        sums.append(jnp.sum(part.T, axis=0, keepdims=True))
    left = left_ref[:, 16:48, :].reshape(1024, 128)
    tails = []
    for l in range(4):
        delta = dot(left, outer_right_ref[l], ((1,), (0,)))
        total = jnp.zeros((8, 128), F32)
        for c in range(32):
            here = slice(56 * c, 56 * c + 56)
            two = jnp.concatenate([delta[32 * c : 32 * c + 32, 0:128], delta[32 * c : 32 * c + 24, 128:256]], axis=0)
            full = outer_ref[l, here, :].astype(F32) + two
            outer_full_ref[l, here, :] = full
            total += jnp.sum((full * full).reshape(7, 8, 128), axis=0)
        total = jnp.sum(total, axis=0, keepdims=True)
        tails += [total[:, 0:64], total[:, 64:128]]
    squares_ref[...] = jnp.concatenate(
        [jnp.concatenate([s, t], axis=1) for s, t in zip(sums, tails)], axis=0
    )


def scale_kernel(
    own_ref, one_ref, two_ref, three_ref, inner_mag_ref, outer_mag_ref, inner_full_ref, outer_full_ref, inner_out, outer_out, inner_buf, outer_buf, sems
):
    scale = lax.rsqrt((own_ref[...] + one_ref[...]) + (two_ref[...] + three_ref[...]) + epsilon)
    mags = jnp.concatenate([inner_mag_ref[i] for i in range(4)], axis=0)
    factor = (scale[:, 0:448] * mags).T
    copies = []
    for m in range(8):
        column = factor[:, m : m + 1]
        inner_buf[m] = (inner_full_ref[m] * column).astype(BF16)
        copies.append(pltpu.make_async_copy(inner_buf.at[m], inner_out.at[m], sems.at[m]))
        copies[-1].start()
        if m % 2:
            l = m // 2
            row = jnp.concatenate([scale[2 * l : 2 * l + 1, 448:512], scale[2 * l + 1 : 2 * l + 2, 448:512]], axis=1)
            row = row * outer_mag_ref[l]
            outer_buf[l] = (outer_full_ref[l] * row).astype(BF16)
            copies.append(pltpu.make_async_copy(outer_buf.at[l], outer_out.at[l], sems.at[8 + l]))
            copies[-1].start()
    for copy in copies:
        copy.wait()


def swapped(value, d):
    return lax.ppermute(value, "row", [(i, i ^ d) for i in range(lax.axis_size("row"))])


def shards(
    inner_base, inner_left, inner_right, inner_mag, outer_base, outer_left, outer_right, outer_mag
):
    cols = lax.axis_size("col")
    inner_base = jnp.swapaxes(inner_base, 3, 4).reshape(8, 448, 512)
    outer_base = outer_base.reshape(4, 1792, 128)
    left, right = pl.pallas_call(
        pack_kernel,
        out_shape=(pltpu.VMEM((cols, 48, 128), BF16), pltpu.VMEM((24, 512), BF16)),
        in_specs=[in_hbm()] * 4,
        out_specs=(whole(),) * 2,
        scratch_shapes=[
            pltpu.VMEM((8, 16, 16), BF16),
            pltpu.VMEM((4, 16, 56), BF16),
            pltpu.VMEM((8, 2, 448), BF16),
            pltpu.VMEM((4, 2, 128), BF16),
            pltpu.SemaphoreType.DMA((4,)),
        ],
        compiler_params=params(4),
        name="pack",
    )(
        kept(inner_left.reshape(8, 16, 16)),
        kept(jnp.swapaxes(outer_left, 2, 3).reshape(4, 16, 56)),
        kept(inner_right.reshape(8, 2, 448)),
        kept(outer_right.reshape(4, 2, 128)),
    )
    partner = swapped(right, 1)
    left = lax.all_to_all(left, "col", 0, 0, tiled=True)
    right = jnp.stack([right, partner])
    far = [swapped(right, d) for d in FAR]
    early = pl.pallas_call(
        load_kernel,
        out_shape=pltpu.VMEM((EARLY, 448, 512), BF16),
        in_specs=[in_hbm()],
        out_specs=whole(),
        scratch_shapes=[pltpu.SemaphoreType.DMA((1,))],
        compiler_params=params(4),
        name="load",
    )(kept(inner_base))
    inner_ranks, outer_ranks = pl.pallas_call(
        gather_right_kernel,
        out_shape=(pltpu.VMEM((448, 128), BF16), pltpu.VMEM((4, 128, 256), BF16)),
        in_specs=[whole()] * 4,
        out_specs=(whole(), whole()),
        scratch_shapes=[pltpu.VMEM((8, 24, 512), F32)],
        compiler_params=params(4),
        name="gather_right",
    )(right, *far)
    inner_full, outer_full, squares = pl.pallas_call(
        squares_kernel,
        out_shape=(
            pltpu.VMEM((8, 448, 512), F32),
            pltpu.VMEM((4, 1792, 128), F32),
            pltpu.VMEM((8, 512), F32),
        ),
        in_specs=[whole()] * 4 + [in_hbm()] * 2,
        out_specs=(whole(),) * 3,
        scratch_shapes=[
            pltpu.VMEM((8 - EARLY, 448, 512), BF16),
            pltpu.VMEM((4, 1792, 128), BF16),
            pltpu.SemaphoreType.DMA((12 - EARLY,)),
        ],
        compiler_params=params(12),
        name="squares",
    )(left, inner_ranks, outer_ranks, early, kept(inner_base), kept(outer_base))
    squares = squares + swapped(squares, 1)
    far = [swapped(squares, d) for d in FAR]
    inner_merged, outer_merged = pl.pallas_call(
        scale_kernel,
        out_shape=(
            jax.ShapeDtypeStruct((8, 448, 512), BF16),
            jax.ShapeDtypeStruct((4, 1792, 128), BF16),
        ),
        in_specs=[whole()] * 8,
        out_specs=(in_hbm(),) * 2,
        scratch_shapes=[
            pltpu.VMEM((8, 448, 512), BF16),
            pltpu.VMEM((4, 1792, 128), BF16),
            pltpu.SemaphoreType.DMA((12,)),
        ],
        compiler_params=params(12),
        name="scale",
    )(squares, *far, inner_mag.reshape(4, 2, 448), outer_mag, inner_full, outer_full)
    inner_merged = jnp.swapaxes(inner_merged.reshape(4, 1, 2, 448, 512), 3, 4)
    return inner_merged, outer_merged.reshape(4, 1, 1792, 128)


def solution(mesh):
    in_specs = (
        P(None, None, None, "row", "col"),
        P(None, None, None, ("row", "col"), None),
        P(None, None, None, "row", "col"),
        P(None, None, None, "col"),
        P(None, None, "row", "col"),
        P(None, None, ("row", "col"), None),
        P(None, None, "row", "col"),
        P(None, None, "col"),
    )
    out_specs = (P(None, None, None, "row", "col"), P(None, None, "row", "col"))
    return jax.shard_map(shards, mesh=mesh, in_specs=in_specs, out_specs=out_specs, check_vma=False)
```

time: 57.6 us -> 44.1 us (0.77)
  blocking collectives: 12.1 us -> 0 us
  starting transfers between devices: 17 us -> 24.6 us
  local copies, waits for them, and re-layouts: 6.41 us -> 0.01 us
  waiting for transfers between devices: 14.2 us -> 9.11 us
  Pallas kernels: 6.68 us -> 9.35 us
    ppermute x0 -> x8, starting transfers between devices: none -> 12.8 us  [swapped(): lax.ppermute(value, 'row', [(i, i ^ d) for i in range(lax.axis_size('row'...]
    all_to_all x2 -> x1, waiting for transfers between devices: 14.2 us -> 1.48 us  [shards(): left = lax.all_to_all(left, 'col', 0, 0, tiled=True)]
    all_to_all x1 -> x0, blocking collectives: 12.1 us -> none  [exchange(): return lax.all_to_all(blocks, axis, 0, 0, tiled=True)]
    ppermute x0 -> x8, waiting for transfers between devices: none -> 7.63 us  [swapped(): lax.ppermute(value, 'row', [(i, i ^ d) for i in range(lax.axis_size('row'...]
    unnamed x16 -> x4, local copies, waits for them, and re-layouts: 6.41 us -> 0.01 us
    all_to_all x2 -> x1, starting transfers between devices: 17 us -> 11.9 us  [shards(): left = lax.all_to_all(left, 'col', 0, 0, tiled=True)]
    pallas_call x3, Pallas kernels: 2.09 us -> 3.74 us  [the longest x1 1.81 us: shards(): pl.pallas_call(pack_kernel, out_shape=(pltpu.VMEM((cols, 48, 128), BF16),...]
    pallas_call x1, Pallas kernels: 1.81 us -> 2.83 us  [shards(): pl.pallas_call(squares_kernel, out_shape=(pltpu.VMEM((8, 448, 512), F32),...]
  transfers between devices with their start and end apart: 2 -> 9, of which waited for: 2 -> 6; matrix products, arithmetic and copies ran while one was open for 0% -> 0% of each run, Pallas kernels for 2% -> 4%
where the time goes in v2:
time: 44.1 us; the launch traced here: 43.8 us
  starting transfers between devices  24.6 us (56%)
  Pallas kernels  9.35 us (21%)
  waiting for transfers between devices  9.11 us (21%)
  between operations  0.69 us (2%)
    ppermute x8, starting transfers between devices, swapped(): lax.ppermute(value, 'row', [(i, i ^ d) for i in range(lax.axis_size('row'...  12.8 us
    all_to_all x1, starting transfers between devices, shards(): left = lax.all_to_all(left, 'col', 0, 0, tiled=True)  11.9 us
    ppermute x8, waiting for transfers between devices, swapped(): lax.ppermute(value, 'row', [(i, i ^ d) for i in range(lax.axis_size('row'...  7.63 us
    pallas_call x1, Pallas kernels, shards(): pl.pallas_call(squares_kernel, out_shape=(pltpu.VMEM((8, 448, 512), F32),...  2.83 us
    pallas_call x1, Pallas kernels, shards(): pl.pallas_call(scale_kernel, out_shape=(jax.ShapeDtypeStruct((8, 448, 512...  2.78 us
    pallas_call x1, Pallas kernels, shards(): pl.pallas_call(pack_kernel, out_shape=(pltpu.VMEM((cols, 48, 128), BF16),...  1.81 us
    pallas_call x1, Pallas kernels, shards(): pl.pallas_call(load_kernel, out_shape=pltpu.VMEM((EARLY, 448, 512), BF16)...  1.79 us
    all_to_all x1, waiting for transfers between devices, shards(): left = lax.all_to_all(left, 'col', 0, 0, tiled=True)  1.48 us
  transfers between devices with their start and end apart: 9, of which 6 were waited for; matrix products, arithmetic and copies ran while one was open for 0% of the time, Pallas kernels for 4%

profile of v2, /device:TPU:1, one launch (start us, length us, event | category | flops | bytes accessed | tf_op | source)
XLA Modules:
  0.0 43.8 jit_solution(7341966179062908284)
XLA Ops:
  0.6 1.8 %pack.1 = (bf16[32,48,128]{2,1,0:T(8,128)(2,1)}, bf16[24,512]{1,0:T(8,128)(2,1)S(1)}) custom-call(bf16[8,16,16]{2,1,0:T(8,128)(2,1)} %bitcast.28, bf16[4,16,56]{2,1,0:T(8,128)(2,1)} %bitcast.30, bf16[8,2,448]{2,1,0:T(2,128)(2,1)} %bitcast.31, bf16[4,2,128]{2,1,0:T(2,128)(2,1)} %bitcast.32), custom_call_target="tpu_custom_call" | custom-call | tf_op jit(solution)/shard_map/pack/pallas_call | solution.py:192
  2.4 11.9 %all-to-all-start = ((bf16[32,48,128]{2,1,0:T(8,128)(2,1)}), bf16[32,48,128]{2,1,0:T(8,128)(2,1)S(1)}, u32[]{:S(2)}, u32[]{:S(2)}) async-start(bf16[32,48,128]{2,1,0:T(8,128)(2,1)} %get-tuple-element.11), calls=%async_computation | async-start | bytes 786432 | tf_op jit(solution)/shard_map/all_to_all | solution.py:213
  14.3 1.0 %collective-permute-start = (bf16[24,512]{1,0:T(8,128)(2,1)S(1)}, bf16[24,512]{1,0:T(8,128)(2,1)S(1)}, u32[]{:S(2)}, u32[]{:S(2)}) collective-permute-start(bf16[24,512]{1,0:T(8,128)(2,1)S(1)} %get-tuple-element.12), channel_id=1, source_target_pairs={{0,32},{32,0},{64,96},{96,64},{128,160},{160,128},{192,224},{224,1... | collective-permute-start | bytes 73736 | tf_op jit(solution)/shard_map/ppermute | solution.py:183
  15.4 0.8 %collective-permute-done = bf16[24,512]{1,0:T(8,128)(2,1)S(1)} collective-permute-done((bf16[24,512]{1,0:T(8,128)(2,1)S(1)}, bf16[24,512]{1,0:T(8,128)(2,1)S(1)}, u32[]{:S(2)}, u32[]{:S(2)}) %collective-permute-start) | collective-permute-done | bytes 24608 | tf_op jit(solution)/shard_map/ppermute | solution.py:183
  16.2 3.1 %collective-permute-start.3 = (bf16[2,24,512]{2,1,0:T(8,128)(2,1)S(1)}, bf16[2,24,512]{2,1,0:T(8,128)(2,1)S(1)}, u32[]{:S(2)}, u32[]{:S(2)}) collective-permute-start(bf16[2,24,512]{2,1,0:T(8,128)(2,1)S(1)} %pad_maximum_fusion.own_ref), channel_id=1, source_target_pairs={{0,160},{32,128},{64,224},{96,192},{128,32},{160,0},{192,96},{224,... | collective-permute-start | bytes 147464 | tf_op jit(solution)/shard_map/ppermute | solution.py:183
  19.4 0.8 %collective-permute-start.2 = (bf16[2,24,512]{2,1,0:T(8,128)(2,1)S(1)}, bf16[2,24,512]{2,1,0:T(8,128)(2,1)S(1)}, u32[]{:S(2)}, u32[]{:S(2)}) collective-permute-start(bf16[2,24,512]{2,1,0:T(8,128)(2,1)S(1)} %pad_maximum_fusion.own_ref), channel_id=1, source_target_pairs={{0,224},{32,192},{64,160},{96,128},{128,96},{160,64},{192,32},{224... | collective-permute-start | bytes 147464 | tf_op jit(solution)/shard_map/ppermute | solution.py:183
  20.2 0.0 collective-permute-start.1
  20.2 1.8 %load.1.early_ref = bf16[6,448,512]{2,1,0:T(8,128)(2,1)S(1)} custom-call(bf16[8,448,512]{2,1,0:T(8,128)(2,1)} %bitcast.25), custom_call_target="tpu_custom_call" | custom-call | tf_op jit(solution)/shard_map/load/pallas_call | solution.py:216
  22.0 0.0 collective-permute-done.3.three_ref
  22.0 2.4 %collective-permute-done.2.two_ref = bf16[2,24,512]{2,1,0:T(8,128)(2,1)S(1)} collective-permute-done((bf16[2,24,512]{2,1,0:T(8,128)(2,1)S(1)}, bf16[2,24,512]{2,1,0:T(8,128)(2,1)S(1)}, u32[]{:S(2)}, u32[]{:S(2)}) %collective-permute-start.2) | collective-permute-done | bytes 49184 | tf_op jit(solution)/shard_map/ppermute | solution.py:183
  24.4 0.0 collective-permute-done.1.one_ref
  24.4 0.1 gather_right.1
  24.5 1.5 %all-to-all-done.left_ref = bf16[32,48,128]{2,1,0:T(8,128)(2,1)S(1)} async-done(((bf16[32,48,128]{2,1,0:T(8,128)(2,1)}), bf16[32,48,128]{2,1,0:T(8,128)(2,1)S(1)}, u32[]{:S(2)}, u32[]{:S(2)}) %all-to-all-start) | async-done | bytes 393248 | tf_op jit(solution)/shard_map/all_to_all | solution.py:213
  26.0 0.0 copy-start
  26.0 0.0 copy-start.1
  26.0 2.8 %squares.1 = (f32[8,448,512]{2,1,0:T(8,128)S(1)}, f32[4,1792,128]{2,1,0:T(8,128)S(1)}, f32[8,512]{1,0:T(8,128)S(1)}) custom-call(bf16[32,48,128]{2,1,0:T(8,128)(2,1)S(1)} %all-to-all-done.left_ref, bf16[448,128]{1,0:T(8,128)(2,1)S(1)} %get-tuple-element.13.inner_right_ref, bf16[4,128,256]{2,1,0:T(8,128)(2,1)S(1)} %get-tuple-element.14.outer_right_ref, ...), custom_call_target="tpu_custom_call" | custom-call | tf_op jit(solution)/shard_map/squares/pallas_call | solution.py:234
  28.9 3.8 %collective-permute-start.4 = (f32[8,512]{1,0:T(8,128)S(1)}, f32[8,512]{1,0:T(8,128)S(1)}, u32[]{:S(2)}, u32[]{:S(2)}) collective-permute-start(f32[8,512]{1,0:T(8,128)S(1)} %get-tuple-element.15), channel_id=1, source_target_pairs={{0,32},{32,0},{64,96},{96,64},{128,160},{160,128},{192,224},{224,1... | collective-permute-start | bytes 49160 | tf_op jit(solution)/shard_map/ppermute | solution.py:183
  32.6 0.8 %collective-permute-done.4 = f32[8,512]{1,0:T(8,128)S(1)} collective-permute-done((f32[8,512]{1,0:T(8,128)S(1)}, f32[8,512]{1,0:T(8,128)S(1)}, u32[]{:S(2)}, u32[]{:S(2)}) %collective-permute-start.4) | collective-permute-done | bytes 16416 | tf_op jit(solution)/shard_map/ppermute | solution.py:183
  33.5 3.1 %collective-permute-start.7 = (f32[8,512]{1,0:T(8,128)S(1)}, f32[8,512]{1,0:T(8,128)S(1)}, u32[]{:S(2)}, u32[]{:S(2)}) collective-permute-start(f32[8,512]{1,0:T(8,128)S(1)} %add.3.own_ref), channel_id=1, source_target_pairs={{0,160},{32,128},{64,224},{96,192},{128,32},{160,0},{192,96},{224,... | collective-permute-start | bytes 49160 | tf_op jit(solution)/shard_map/ppermute | solution.py:183
  36.6 0.8 %collective-permute-start.6 = (f32[8,512]{1,0:T(8,128)S(1)}, f32[8,512]{1,0:T(8,128)S(1)}, u32[]{:S(2)}, u32[]{:S(2)}) collective-permute-start(f32[8,512]{1,0:T(8,128)S(1)} %add.3.own_ref), channel_id=1, source_target_pairs={{0,224},{32,192},{64,160},{96,128},{128,96},{160,64},{192,32},{224... | collective-permute-start | bytes 49160 | tf_op jit(solution)/shard_map/ppermute | solution.py:183
  37.5 0.0 collective-permute-start.5
  37.5 0.7 %collective-permute-done.7.three_ref = f32[8,512]{1,0:T(8,128)S(1)} collective-permute-done((f32[8,512]{1,0:T(8,128)S(1)}, f32[8,512]{1,0:T(8,128)S(1)}, u32[]{:S(2)}, u32[]{:S(2)}) %collective-permute-start.7) | collective-permute-done | bytes 16416 | tf_op jit(solution)/shard_map/ppermute | solution.py:183
  38.2 2.9 %collective-permute-done.6.two_ref = f32[8,512]{1,0:T(8,128)S(1)} collective-permute-done((f32[8,512]{1,0:T(8,128)S(1)}, f32[8,512]{1,0:T(8,128)S(1)}, u32[]{:S(2)}, u32[]{:S(2)}) %collective-permute-start.6) | collective-permute-done | bytes 16416 | tf_op jit(solution)/shard_map/ppermute | solution.py:183
  41.0 0.0 collective-permute-done.5.one_ref
  41.0 0.0 copy-done
  41.0 0.0 copy-done.1
  41.0 2.8 %scale.1 = (bf16[8,448,512]{2,1,0:T(8,128)(2,1)}, bf16[4,1792,128]{2,1,0:T(8,128)(2,1)}) custom-call(f32[8,512]{1,0:T(8,128)S(1)} %add.3.own_ref, f32[8,512]{1,0:T(8,128)S(1)} %collective-permute-done.5.one_ref, f32[8,512]{1,0:T(8,128)S(1)} %collective-permute-done.6.two_ref, f32[8,512]{1,0:T(8,128)S(1)} %collective-permute-done.7.three_ref, ...), custom_call_target="tpu_custom_call" | custom-call | tf_op jit(solution)/shard_map/scale/pallas_call | solution.py:253
  (2 shorter events, 0.0 us)
Async XLA Ops:
  2.4 23.6 %all-to-all-start = ((bf16[32,48,128]{2,1,0:T(8,128)(2,1)}), bf16[32,48,128]{2,1,0:T(8,128)(2,1)S(1)}, u32[]{:S(2)}, u32[]{:S(2)}) async-start(bf16[32,48,128]{2,1,0:T(8,128)(2,1)} %get-tuple-element.11), calls=%async_computation | async-start | bytes 786432 | tf_op jit(solution)/shard_map/all_to_all | solution.py:213
  14.3 1.9 %collective-permute-start = (bf16[24,512]{1,0:T(8,128)(2,1)S(1)}, bf16[24,512]{1,0:T(8,128)(2,1)S(1)}, u32[]{:S(2)}, u32[]{:S(2)}) collective-permute-start(bf16[24,512]{1,0:T(8,128)(2,1)S(1)} %get-tuple-element.12), channel_id=1, source_target_pairs={{0,32},{32,0},{64,96},{96,64},{128,160},{160,128},{192,224},{224,1... | collective-permute-start | bytes 73736 | tf_op jit(solution)/shard_map/ppermute | solution.py:183
  16.2 5.8 %collective-permute-start.3 = (bf16[2,24,512]{2,1,0:T(8,128)(2,1)S(1)}, bf16[2,24,512]{2,1,0:T(8,128)(2,1)S(1)}, u32[]{:S(2)}, u32[]{:S(2)}) collective-permute-start(bf16[2,24,512]{2,1,0:T(8,128)(2,1)S(1)} %pad_maximum_fusion.own_ref), channel_id=1, source_target_pairs={{0,160},{32,128},{64,224},{96,192},{128,32},{160,0},{192,96},{224,... | collective-permute-start | bytes 147464 | tf_op jit(solution)/shard_map/ppermute | solution.py:183
  19.4 5.0 %collective-permute-start.2 = (bf16[2,24,512]{2,1,0:T(8,128)(2,1)S(1)}, bf16[2,24,512]{2,1,0:T(8,128)(2,1)S(1)}, u32[]{:S(2)}, u32[]{:S(2)}) collective-permute-start(bf16[2,24,512]{2,1,0:T(8,128)(2,1)S(1)} %pad_maximum_fusion.own_ref), channel_id=1, source_target_pairs={{0,224},{32,192},{64,160},{96,128},{128,96},{160,64},{192,32},{224... | collective-permute-start | bytes 147464 | tf_op jit(solution)/shard_map/ppermute | solution.py:183
  20.2 4.2 %collective-permute-start.1 = (bf16[2,24,512]{2,1,0:T(8,128)(2,1)S(1)}, bf16[2,24,512]{2,1,0:T(8,128)(2,1)S(1)}, u32[]{:S(2)}, u32[]{:S(2)}) collective-permute-start(bf16[2,24,512]{2,1,0:T(8,128)(2,1)S(1)} %pad_maximum_fusion.own_ref), channel_id=1, source_target_pairs={{0,96},{32,64},{64,32},{96,0},{128,224},{160,192},{192,160},{224,1... | collective-permute-start | bytes 147464 | tf_op jit(solution)/shard_map/ppermute | solution.py:183
  26.0 15.0 %copy-start = (f32[4,1,2,448]{3,2,1,0:T(2,128)S(1)}, f32[4,1,2,448]{3,2,1,0:T(2,128)}, u32[]{:S(2)}) copy-start(f32[4,1,2,448]{3,2,1,0:T(2,128)} %param.11) | copy-start | bytes 43012
  26.0 15.0 %copy-start.1 = (f32[4,1,128]{2,1,0:T(1,128)S(1)}, f32[4,1,128]{2,1,0:T(1,128)}, u32[]{:S(2)}) copy-start(f32[4,1,128]{2,1,0:T(1,128)} %outer_mag_ref.1) | copy-start | bytes 6148
  28.9 4.6 %collective-permute-start.4 = (f32[8,512]{1,0:T(8,128)S(1)}, f32[8,512]{1,0:T(8,128)S(1)}, u32[]{:S(2)}, u32[]{:S(2)}) collective-permute-start(f32[8,512]{1,0:T(8,128)S(1)} %get-tuple-element.15), channel_id=1, source_target_pairs={{0,32},{32,0},{64,96},{96,64},{128,160},{160,128},{192,224},{224,1... | collective-permute-start | bytes 49160 | tf_op jit(solution)/shard_map/ppermute | solution.py:183
  33.5 4.7 %collective-permute-start.7 = (f32[8,512]{1,0:T(8,128)S(1)}, f32[8,512]{1,0:T(8,128)S(1)}, u32[]{:S(2)}, u32[]{:S(2)}) collective-permute-start(f32[8,512]{1,0:T(8,128)S(1)} %add.3.own_ref), channel_id=1, source_target_pairs={{0,160},{32,128},{64,224},{96,192},{128,32},{160,0},{192,96},{224,... | collective-permute-start | bytes 49160 | tf_op jit(solution)/shard_map/ppermute | solution.py:183
  36.6 4.4 %collective-permute-start.6 = (f32[8,512]{1,0:T(8,128)S(1)}, f32[8,512]{1,0:T(8,128)S(1)}, u32[]{:S(2)}, u32[]{:S(2)}) collective-permute-start(f32[8,512]{1,0:T(8,128)S(1)} %add.3.own_ref), channel_id=1, source_target_pairs={{0,224},{32,192},{64,160},{96,128},{128,96},{160,64},{192,32},{224... | collective-permute-start | bytes 49160 | tf_op jit(solution)/shard_map/ppermute | solution.py:183
  37.5 3.6 %collective-permute-start.5 = (f32[8,512]{1,0:T(8,128)S(1)}, f32[8,512]{1,0:T(8,128)S(1)}, u32[]{:S(2)}, u32[]{:S(2)}) collective-permute-start(f32[8,512]{1,0:T(8,128)S(1)} %add.3.own_ref), channel_id=1, source_target_pairs={{0,96},{32,64},{64,32},{96,0},{128,224},{160,192},{192,160},{224,1... | collective-permute-start | bytes 49160 | tf_op jit(solution)/shard_map/ppermute | solution.py:183

commit v3 on v2

--- a/solution.py
+++ b/solution.py
@@ -47,7 +47,7 @@
 
 def pack_kernel(
     inner_left_hbm, outer_left_hbm, inner_right_hbm, outer_right_hbm, left_out, right_out,
-    inner_left_ref, outer_left_ref, inner_right_ref, outer_right_ref, sems
+    inner_left_ref, outer_left_ref, inner_right_ref, outer_right_ref, left_ref, sems
 ):
     fetch(
         [
@@ -72,8 +72,10 @@
     first = outer[0:32, 0:128]
     second = jnp.concatenate([outer[32:56, 128:256], jnp.zeros((8, 128), F32)], axis=0)
     block = jnp.concatenate([inner, first + second], axis=0).astype(BF16)
-    for i in range(left_out.shape[0]):
-        left_out[i] = block
+    for i in range(left_ref.shape[0]):
+        left_ref[i] = block
+    sent = pltpu.make_async_copy(left_ref, left_out, sems.at[4])
+    sent.start()
     row, e = iota((16, 2), 0), iota((16, 2), 1)
     inner = jnp.zeros((16, 448), F32)
     for m in range(8):
@@ -84,9 +86,9 @@
     for l in range(4):
         pick = (row == 2 * l + e).astype(F32).astype(BF16)
         outer += dot(pick, outer_right_ref[l], ((1,), (0,)))
-    inner = jnp.concatenate([inner, jnp.zeros((16, 64), F32)], axis=1)
-    outer = jnp.concatenate([outer, jnp.zeros((8, 384), F32)], axis=1)
-    right_out[...] = jnp.concatenate([inner, outer], axis=0).astype(BF16)
+    outer = jnp.concatenate([outer[:, 0:64], outer[:, 64:128]], axis=0)
+    right_out[...] = jnp.concatenate([inner, outer], axis=1).astype(BF16)
+    sent.wait()
 
 
 def gather_right_kernel(own_ref, one_ref, two_ref, three_ref, inner_ref, outer_ref, right_ref):
@@ -94,8 +96,8 @@
     for d, ref in zip((0, *FAR), (own_ref, one_ref, two_ref, three_ref)):
         for core in range(2):
             right_ref[me ^ (d ^ core)] = ref[core].astype(F32)
-    inner_ref[...] = right_ref[:, 0:16, :].reshape(128, 512).T[0:448, :].astype(BF16)
-    ranks = right_ref[:, 16:24, 0:128].reshape(64, 128)
+    inner_ref[...] = right_ref[...].reshape(128, 512).T[0:448, :].astype(BF16)
+    ranks = jnp.concatenate([right_ref[:, 0:8, 448:512], right_ref[:, 8:16, 448:512]], axis=2).reshape(64, 128)
     matrix = (iota((64, 128), 0) % 8) // 2
     zero = jnp.zeros((64, 128), F32)
     for l in range(4):
@@ -121,16 +123,15 @@
         return carry
 
     lax.fori_loop(0, 8 - EARLY, start_inner, 0)
-    lax.fori_loop(0, 4, start_outer, 0)
     left = left_ref[:, 0:16, :].reshape(512, 128)
     matrix = (iota((1, 128), 1) % 16) // 2
     sums = []
     for m in range(8):
+        if m == 1:
+            lax.fori_loop(0, 4, start_outer, 0)
         if m == EARLY:
             for i in range(8 - EARLY):
                 pltpu.make_async_copy(inner_hbm.at[EARLY + i], late_ref.at[i], sems.at[i]).wait()
-            for l in range(4):
-                pltpu.make_async_copy(outer_hbm.at[l], outer_ref.at[l], sems.at[8 - EARLY + l]).wait()
         base = early_ref[m] if m < EARLY else late_ref[m - EARLY]
         right = inner_right_ref[...] * (matrix == m).astype(F32).astype(BF16)
         full = base.astype(F32) + dot(right, left, ((1,), (1,)))
@@ -140,6 +141,8 @@
         sums.append(jnp.sum(part.T, axis=0, keepdims=True))
     left = left_ref[:, 16:48, :].reshape(1024, 128)
     tails = []
+    for l in range(4):
+        pltpu.make_async_copy(outer_hbm.at[l], outer_ref.at[l], sems.at[8 - EARLY + l]).wait()
     for l in range(4):
         delta = dot(left, outer_right_ref[l], ((1,), (0,)))
         total = jnp.zeros((8, 128), F32)
@@ -159,24 +162,38 @@
 def scale_kernel(
     own_ref, one_ref, two_ref, three_ref, inner_mag_ref, outer_mag_ref, inner_full_ref, outer_full_ref, inner_out, outer_out, inner_buf, outer_buf, sems
 ):
+    here = lax.axis_index("row")
     scale = lax.rsqrt((own_ref[...] + one_ref[...]) + (two_ref[...] + three_ref[...]) + epsilon)
     mags = jnp.concatenate([inner_mag_ref[i] for i in range(4)], axis=0)
     factor = (scale[:, 0:448] * mags).T
-    copies = []
+
+    def sent_outer(l):
+        return pltpu.make_async_copy(outer_buf.at[l], outer_out.at[l], sems.at[8 + l])
+
+    def sent_inner(m):
+        return pltpu.make_async_copy(inner_buf.at[m], inner_out.at[m], sems.at[m])
+
+    for l in range(4):
+        row = jnp.concatenate([scale[2 * l : 2 * l + 1, 448:512], scale[2 * l + 1 : 2 * l + 2, 448:512]], axis=1)
+        row = row * outer_mag_ref[l]
+
+        @pl.when(here >= 0)
+        def _():
+            outer_buf[l] = (outer_full_ref[l] * row).astype(BF16)
+            sent_outer(l).start()
+
     for m in range(8):
         column = factor[:, m : m + 1]
-        inner_buf[m] = (inner_full_ref[m] * column).astype(BF16)
-        copies.append(pltpu.make_async_copy(inner_buf.at[m], inner_out.at[m], sems.at[m]))
-        copies[-1].start()
-        if m % 2:
-            l = m // 2
-            row = jnp.concatenate([scale[2 * l : 2 * l + 1, 448:512], scale[2 * l + 1 : 2 * l + 2, 448:512]], axis=1)
-            row = row * outer_mag_ref[l]
-            outer_buf[l] = (outer_full_ref[l] * row).astype(BF16)
-            copies.append(pltpu.make_async_copy(outer_buf.at[l], outer_out.at[l], sems.at[8 + l]))
-            copies[-1].start()
-    for copy in copies:
-        copy.wait()
+
+        @pl.when(here >= 0)
+        def _():
+            inner_buf[m] = (inner_full_ref[m] * column).astype(BF16)
+            sent_inner(m).start()
+
+    for l in range(4):
+        sent_outer(l).wait()
+    for m in range(8):
+        sent_inner(m).wait()
 
 
 def swapped(value, d):
@@ -191,15 +208,16 @@
     outer_base = outer_base.reshape(4, 1792, 128)
     left, right = pl.pallas_call(
         pack_kernel,
-        out_shape=(pltpu.VMEM((cols, 48, 128), BF16), pltpu.VMEM((24, 512), BF16)),
+        out_shape=(jax.ShapeDtypeStruct((cols, 48, 128), BF16), pltpu.VMEM((16, 512), BF16)),
         in_specs=[in_hbm()] * 4,
-        out_specs=(whole(),) * 2,
+        out_specs=(in_hbm(), whole()),
         scratch_shapes=[
             pltpu.VMEM((8, 16, 16), BF16),
             pltpu.VMEM((4, 16, 56), BF16),
             pltpu.VMEM((8, 2, 448), BF16),
             pltpu.VMEM((4, 2, 128), BF16),
-            pltpu.SemaphoreType.DMA((4,)),
+            pltpu.VMEM((cols, 48, 128), BF16),
+            pltpu.SemaphoreType.DMA((5,)),
         ],
         compiler_params=params(4),
         name="pack",
@@ -227,7 +245,7 @@
         out_shape=(pltpu.VMEM((448, 128), BF16), pltpu.VMEM((4, 128, 256), BF16)),
         in_specs=[whole()] * 4,
         out_specs=(whole(), whole()),
-        scratch_shapes=[pltpu.VMEM((8, 24, 512), F32)],
+        scratch_shapes=[pltpu.VMEM((8, 16, 512), F32)],
         compiler_params=params(4),
         name="gather_right",
     )(right, *far)

time: 44.1 us -> 43.9 us (level)
  no operation moved by 1% of the time
where the time goes in v3:
time: 43.9 us; the launch traced here: 43.6 us
  starting transfers between devices  24.6 us (56%)
  Pallas kernels  9.2 us (21%)
  waiting for transfers between devices  9.1 us (21%)
  between operations  0.69 us (2%)
    ppermute x8, starting transfers between devices, swapped(): lax.ppermute(value, 'row', [(i, i ^ d) for i in range(lax.axis_size('row'...  12.8 us
    all_to_all x1, starting transfers between devices, shards(): left = lax.all_to_all(left, 'col', 0, 0, tiled=True)  11.9 us
    ppermute x8, waiting for transfers between devices, swapped(): lax.ppermute(value, 'row', [(i, i ^ d) for i in range(lax.axis_size('row'...  7.44 us
    pallas_call x1, Pallas kernels, shards(): pl.pallas_call(scale_kernel, out_shape=(jax.ShapeDtypeStruct((8, 448, 512...  2.73 us
    pallas_call x1, Pallas kernels, shards(): pl.pallas_call(squares_kernel, out_shape=(pltpu.VMEM((8, 448, 512), F32),...  2.71 us
    pallas_call x1, Pallas kernels, shards(): pl.pallas_call(pack_kernel, out_shape=(jax.ShapeDtypeStruct((cols, 48, 12...  1.8 us
    pallas_call x1, Pallas kernels, shards(): pl.pallas_call(load_kernel, out_shape=pltpu.VMEM((EARLY, 448, 512), BF16)...  1.79 us
    all_to_all x1, waiting for transfers between devices, shards(): left = lax.all_to_all(left, 'col', 0, 0, tiled=True)  1.66 us
  transfers between devices with their start and end apart: 9, of which 6 were waited for; matrix products, arithmetic and copies ran while one was open for 0% of the time, Pallas kernels for 4%

profile of v3, /device:TPU:1, one launch (start us, length us, event | category | flops | bytes accessed | tf_op | source)
XLA Modules:
  0.0 43.6 jit_solution(14585961453236693545)
XLA Ops:
  0.6 1.8 %pack.1 = (bf16[32,48,128]{2,1,0:T(8,128)(2,1)}, bf16[16,512]{1,0:T(8,128)(2,1)S(1)}) custom-call(bf16[8,16,16]{2,1,0:T(8,128)(2,1)} %bitcast.28, bf16[4,16,56]{2,1,0:T(8,128)(2,1)} %bitcast.29, bf16[8,2,448]{2,1,0:T(2,128)(2,1)} %bitcast.30, bf16[4,2,128]{2,1,0:T(2,128)(2,1)} %bitcast.32), custom_call_target="tpu_custom_call" | custom-call | tf_op jit(solution)/shard_map/pack/pallas_call | solution.py:209
  2.4 11.9 %all-to-all-start = ((bf16[32,48,128]{2,1,0:T(8,128)(2,1)}), bf16[32,48,128]{2,1,0:T(8,128)(2,1)S(1)}, u32[]{:S(2)}, u32[]{:S(2)}) async-start(bf16[32,48,128]{2,1,0:T(8,128)(2,1)} %get-tuple-element.11), calls=%async_computation | async-start | bytes 786432 | tf_op jit(solution)/shard_map/all_to_all | solution.py:231
  14.3 1.0 %collective-permute-start = (bf16[16,512]{1,0:T(8,128)(2,1)S(1)}, bf16[16,512]{1,0:T(8,128)(2,1)S(1)}, u32[]{:S(2)}, u32[]{:S(2)}) collective-permute-start(bf16[16,512]{1,0:T(8,128)(2,1)S(1)} %get-tuple-element.12), channel_id=1, source_target_pairs={{0,32},{32,0},{64,96},{96,64},{128,160},{160,128},{192,224},{224,1... | collective-permute-start | bytes 49160 | tf_op jit(solution)/shard_map/ppermute | solution.py:200
  15.4 0.8 %collective-permute-done = bf16[16,512]{1,0:T(8,128)(2,1)S(1)} collective-permute-done((bf16[16,512]{1,0:T(8,128)(2,1)S(1)}, bf16[16,512]{1,0:T(8,128)(2,1)S(1)}, u32[]{:S(2)}, u32[]{:S(2)}) %collective-permute-start) | collective-permute-done | bytes 16416 | tf_op jit(solution)/shard_map/ppermute | solution.py:200
  16.2 3.1 %collective-permute-start.3 = (bf16[2,16,512]{2,1,0:T(8,128)(2,1)S(1)}, bf16[2,16,512]{2,1,0:T(8,128)(2,1)S(1)}, u32[]{:S(2)}, u32[]{:S(2)}) collective-permute-start(bf16[2,16,512]{2,1,0:T(8,128)(2,1)S(1)} %pad_maximum_fusion.own_ref), channel_id=1, source_target_pairs={{0,160},{32,128},{64,224},{96,192},{128,32},{160,0},{192,96},{224,... | collective-permute-start | bytes 98312 | tf_op jit(solution)/shard_map/ppermute | solution.py:200
  19.3 0.8 %collective-permute-start.2 = (bf16[2,16,512]{2,1,0:T(8,128)(2,1)S(1)}, bf16[2,16,512]{2,1,0:T(8,128)(2,1)S(1)}, u32[]{:S(2)}, u32[]{:S(2)}) collective-permute-start(bf16[2,16,512]{2,1,0:T(8,128)(2,1)S(1)} %pad_maximum_fusion.own_ref), channel_id=1, source_target_pairs={{0,224},{32,192},{64,160},{96,128},{128,96},{160,64},{192,32},{224... | collective-permute-start | bytes 98312 | tf_op jit(solution)/shard_map/ppermute | solution.py:200
  20.2 0.0 collective-permute-start.1
  20.2 1.8 %load.1.early_ref = bf16[6,448,512]{2,1,0:T(8,128)(2,1)S(1)} custom-call(bf16[8,448,512]{2,1,0:T(8,128)(2,1)} %bitcast.25), custom_call_target="tpu_custom_call" | custom-call | tf_op jit(solution)/shard_map/load/pallas_call | solution.py:234
  22.0 0.0 collective-permute-done.3.three_ref
  22.0 2.2 %collective-permute-done.2.two_ref = bf16[2,16,512]{2,1,0:T(8,128)(2,1)S(1)} collective-permute-done((bf16[2,16,512]{2,1,0:T(8,128)(2,1)S(1)}, bf16[2,16,512]{2,1,0:T(8,128)(2,1)S(1)}, u32[]{:S(2)}, u32[]{:S(2)}) %collective-permute-start.2) | collective-permute-done | bytes 32800 | tf_op jit(solution)/shard_map/ppermute | solution.py:200
  24.2 0.0 collective-permute-done.1.one_ref
  24.2 0.2 gather_right.1
  24.4 1.7 %all-to-all-done.left_ref = bf16[32,48,128]{2,1,0:T(8,128)(2,1)S(1)} async-done(((bf16[32,48,128]{2,1,0:T(8,128)(2,1)}), bf16[32,48,128]{2,1,0:T(8,128)(2,1)S(1)}, u32[]{:S(2)}, u32[]{:S(2)}) %all-to-all-start) | async-done | bytes 393248 | tf_op jit(solution)/shard_map/all_to_all | solution.py:231
  26.0 0.0 copy-start
  26.0 0.0 copy-start.1
  26.0 2.7 %squares.1 = (f32[8,448,512]{2,1,0:T(8,128)S(1)}, f32[4,1792,128]{2,1,0:T(8,128)S(1)}, f32[8,512]{1,0:T(8,128)S(1)}) custom-call(bf16[32,48,128]{2,1,0:T(8,128)(2,1)S(1)} %all-to-all-done.left_ref, bf16[448,128]{1,0:T(8,128)(2,1)S(1)} %get-tuple-element.13.inner_right_ref, bf16[4,128,256]{2,1,0:T(8,128)(2,1)S(1)} %get-tuple-element.14.outer_right_ref, ...), custom_call_target="tpu_custom_call" | custom-call | tf_op jit(solution)/shard_map/squares/pallas_call | solution.py:252
  28.8 3.8 %collective-permute-start.4 = (f32[8,512]{1,0:T(8,128)S(1)}, f32[8,512]{1,0:T(8,128)S(1)}, u32[]{:S(2)}, u32[]{:S(2)}) collective-permute-start(f32[8,512]{1,0:T(8,128)S(1)} %get-tuple-element.15), channel_id=1, source_target_pairs={{0,32},{32,0},{64,96},{96,64},{128,160},{160,128},{192,224},{224,1... | collective-permute-start | bytes 49160 | tf_op jit(solution)/shard_map/ppermute | solution.py:200
  32.5 0.8 %collective-permute-done.4 = f32[8,512]{1,0:T(8,128)S(1)} collective-permute-done((f32[8,512]{1,0:T(8,128)S(1)}, f32[8,512]{1,0:T(8,128)S(1)}, u32[]{:S(2)}, u32[]{:S(2)}) %collective-permute-start.4) | collective-permute-done | bytes 16416 | tf_op jit(solution)/shard_map/ppermute | solution.py:200
  33.4 3.1 %collective-permute-start.7 = (f32[8,512]{1,0:T(8,128)S(1)}, f32[8,512]{1,0:T(8,128)S(1)}, u32[]{:S(2)}, u32[]{:S(2)}) collective-permute-start(f32[8,512]{1,0:T(8,128)S(1)} %add.3.own_ref), channel_id=1, source_target_pairs={{0,160},{32,128},{64,224},{96,192},{128,32},{160,0},{192,96},{224,... | collective-permute-start | bytes 49160 | tf_op jit(solution)/shard_map/ppermute | solution.py:200
  36.5 0.8 %collective-permute-start.6 = (f32[8,512]{1,0:T(8,128)S(1)}, f32[8,512]{1,0:T(8,128)S(1)}, u32[]{:S(2)}, u32[]{:S(2)}) collective-permute-start(f32[8,512]{1,0:T(8,128)S(1)} %add.3.own_ref), channel_id=1, source_target_pairs={{0,224},{32,192},{64,160},{96,128},{128,96},{160,64},{192,32},{224... | collective-permute-start | bytes 49160 | tf_op jit(solution)/shard_map/ppermute | solution.py:200
  37.3 0.0 collective-permute-start.5
  37.3 0.7 %collective-permute-done.7.three_ref = f32[8,512]{1,0:T(8,128)S(1)} collective-permute-done((f32[8,512]{1,0:T(8,128)S(1)}, f32[8,512]{1,0:T(8,128)S(1)}, u32[]{:S(2)}, u32[]{:S(2)}) %collective-permute-start.7) | collective-permute-done | bytes 16416 | tf_op jit(solution)/shard_map/ppermute | solution.py:200
  38.0 2.8 %collective-permute-done.6.two_ref = f32[8,512]{1,0:T(8,128)S(1)} collective-permute-done((f32[8,512]{1,0:T(8,128)S(1)}, f32[8,512]{1,0:T(8,128)S(1)}, u32[]{:S(2)}, u32[]{:S(2)}) %collective-permute-start.6) | collective-permute-done | bytes 16416 | tf_op jit(solution)/shard_map/ppermute | solution.py:200
  40.9 0.0 collective-permute-done.5.one_ref
  40.9 0.0 copy-done
  40.9 0.0 copy-done.1
  40.9 2.7 %scale.1 = (bf16[8,448,512]{2,1,0:T(8,128)(2,1)}, bf16[4,1792,128]{2,1,0:T(8,128)(2,1)}) custom-call(f32[8,512]{1,0:T(8,128)S(1)} %add.3.own_ref, f32[8,512]{1,0:T(8,128)S(1)} %collective-permute-done.5.one_ref, f32[8,512]{1,0:T(8,128)S(1)} %collective-permute-done.6.two_ref, f32[8,512]{1,0:T(8,128)S(1)} %collective-permute-done.7.three_ref, ...), custom_call_target="tpu_custom_call" | custom-call | tf_op jit(solution)/shard_map/scale/pallas_call | solution.py:271
  (2 shorter events, 0.0 us)
Async XLA Ops:
  2.4 23.6 %all-to-all-start = ((bf16[32,48,128]{2,1,0:T(8,128)(2,1)}), bf16[32,48,128]{2,1,0:T(8,128)(2,1)S(1)}, u32[]{:S(2)}, u32[]{:S(2)}) async-start(bf16[32,48,128]{2,1,0:T(8,128)(2,1)} %get-tuple-element.11), calls=%async_computation | async-start | bytes 786432 | tf_op jit(solution)/shard_map/all_to_all | solution.py:231
  14.3 1.9 %collective-permute-start = (bf16[16,512]{1,0:T(8,128)(2,1)S(1)}, bf16[16,512]{1,0:T(8,128)(2,1)S(1)}, u32[]{:S(2)}, u32[]{:S(2)}) collective-permute-start(bf16[16,512]{1,0:T(8,128)(2,1)S(1)} %get-tuple-element.12), channel_id=1, source_target_pairs={{0,32},{32,0},{64,96},{96,64},{128,160},{160,128},{192,224},{224,1... | collective-permute-start | bytes 49160 | tf_op jit(solution)/shard_map/ppermute | solution.py:200
  16.2 5.8 %collective-permute-start.3 = (bf16[2,16,512]{2,1,0:T(8,128)(2,1)S(1)}, bf16[2,16,512]{2,1,0:T(8,128)(2,1)S(1)}, u32[]{:S(2)}, u32[]{:S(2)}) collective-permute-start(bf16[2,16,512]{2,1,0:T(8,128)(2,1)S(1)} %pad_maximum_fusion.own_ref), channel_id=1, source_target_pairs={{0,160},{32,128},{64,224},{96,192},{128,32},{160,0},{192,96},{224,... | collective-permute-start | bytes 98312 | tf_op jit(solution)/shard_map/ppermute | solution.py:200
  19.3 4.8 %collective-permute-start.2 = (bf16[2,16,512]{2,1,0:T(8,128)(2,1)S(1)}, bf16[2,16,512]{2,1,0:T(8,128)(2,1)S(1)}, u32[]{:S(2)}, u32[]{:S(2)}) collective-permute-start(bf16[2,16,512]{2,1,0:T(8,128)(2,1)S(1)} %pad_maximum_fusion.own_ref), channel_id=1, source_target_pairs={{0,224},{32,192},{64,160},{96,128},{128,96},{160,64},{192,32},{224... | collective-permute-start | bytes 98312 | tf_op jit(solution)/shard_map/ppermute | solution.py:200
  20.2 4.0 %collective-permute-start.1 = (bf16[2,16,512]{2,1,0:T(8,128)(2,1)S(1)}, bf16[2,16,512]{2,1,0:T(8,128)(2,1)S(1)}, u32[]{:S(2)}, u32[]{:S(2)}) collective-permute-start(bf16[2,16,512]{2,1,0:T(8,128)(2,1)S(1)} %pad_maximum_fusion.own_ref), channel_id=1, source_target_pairs={{0,96},{32,64},{64,32},{96,0},{128,224},{160,192},{192,160},{224,1... | collective-permute-start | bytes 98312 | tf_op jit(solution)/shard_map/ppermute | solution.py:200
  26.0 14.9 %copy-start = (f32[4,1,2,448]{3,2,1,0:T(2,128)S(1)}, f32[4,1,2,448]{3,2,1,0:T(2,128)}, u32[]{:S(2)}) copy-start(f32[4,1,2,448]{3,2,1,0:T(2,128)} %param.11) | copy-start | bytes 43012
  26.0 14.9 %copy-start.1 = (f32[4,1,128]{2,1,0:T(1,128)S(1)}, f32[4,1,128]{2,1,0:T(1,128)}, u32[]{:S(2)}) copy-start(f32[4,1,128]{2,1,0:T(1,128)} %outer_mag_ref.1) | copy-start | bytes 6148
  28.8 4.6 %collective-permute-start.4 = (f32[8,512]{1,0:T(8,128)S(1)}, f32[8,512]{1,0:T(8,128)S(1)}, u32[]{:S(2)}, u32[]{:S(2)}) collective-permute-start(f32[8,512]{1,0:T(8,128)S(1)} %get-tuple-element.15), channel_id=1, source_target_pairs={{0,32},{32,0},{64,96},{96,64},{128,160},{160,128},{192,224},{224,1... | collective-permute-start | bytes 49160 | tf_op jit(solution)/shard_map/ppermute | solution.py:200
  33.4 4.7 %collective-permute-start.7 = (f32[8,512]{1,0:T(8,128)S(1)}, f32[8,512]{1,0:T(8,128)S(1)}, u32[]{:S(2)}, u32[]{:S(2)}) collective-permute-start(f32[8,512]{1,0:T(8,128)S(1)} %add.3.own_ref), channel_id=1, source_target_pairs={{0,160},{32,128},{64,224},{96,192},{128,32},{160,0},{192,96},{224,... | collective-permute-start | bytes 49160 | tf_op jit(solution)/shard_map/ppermute | solution.py:200
  36.5 4.4 %collective-permute-start.6 = (f32[8,512]{1,0:T(8,128)S(1)}, f32[8,512]{1,0:T(8,128)S(1)}, u32[]{:S(2)}, u32[]{:S(2)}) collective-permute-start(f32[8,512]{1,0:T(8,128)S(1)} %add.3.own_ref), channel_id=1, source_target_pairs={{0,224},{32,192},{64,160},{96,128},{128,96},{160,64},{192,32},{224... | collective-permute-start | bytes 49160 | tf_op jit(solution)/shard_map/ppermute | solution.py:200
  37.3 3.5 %collective-permute-start.5 = (f32[8,512]{1,0:T(8,128)S(1)}, f32[8,512]{1,0:T(8,128)S(1)}, u32[]{:S(2)}, u32[]{:S(2)}) collective-permute-start(f32[8,512]{1,0:T(8,128)S(1)} %add.3.own_ref), channel_id=1, source_target_pairs={{0,96},{32,64},{64,32},{96,0},{128,224},{160,192},{192,160},{224,1... | collective-permute-start | bytes 49160 | tf_op jit(solution)/shard_map/ppermute | solution.py:200

commit v4 on v3

--- a/solution.py
+++ b/solution.py
@@ -69,11 +69,10 @@
         at = 8 * (k // 2) + 2 * l + k % 2
         pick = jnp.logical_or(lane == at, lane == at + 192).astype(F32).astype(BF16)
         outer += dot(outer_left_ref[l], pick, ((0,), (0,)))
-    first = outer[0:32, 0:128]
-    second = jnp.concatenate([outer[32:56, 128:256], jnp.zeros((8, 128), F32)], axis=0)
-    block = jnp.concatenate([inner, first + second], axis=0).astype(BF16)
+    first, second = outer[:, 0:128], outer[:, 128:256]
+    block = jnp.concatenate([inner, first[0:24] + second[24:48], first[48:52] + second[52:56]], axis=0)
     for i in range(left_ref.shape[0]):
-        left_ref[i] = block
+        left_ref[i] = block.reshape(11, 4, 128).astype(BF16)
     sent = pltpu.make_async_copy(left_ref, left_out, sems.at[4])
     sent.start()
     row, e = iota((16, 2), 0), iota((16, 2), 1)
@@ -123,12 +122,11 @@
         return carry
 
     lax.fori_loop(0, 8 - EARLY, start_inner, 0)
-    left = left_ref[:, 0:16, :].reshape(512, 128)
+    lax.fori_loop(0, 4, start_outer, 0)
+    left = left_ref[:, 0:4].astype(F32).reshape(512, 128).astype(BF16)
     matrix = (iota((1, 128), 1) % 16) // 2
     sums = []
     for m in range(8):
-        if m == 1:
-            lax.fori_loop(0, 4, start_outer, 0)
         if m == EARLY:
             for i in range(8 - EARLY):
                 pltpu.make_async_copy(inner_hbm.at[EARLY + i], late_ref.at[i], sems.at[i]).wait()
@@ -139,7 +137,9 @@
         square = full * full
         part = (square[:, 0:128] + square[:, 128:256]) + (square[:, 256:384] + square[:, 384:512])
         sums.append(jnp.sum(part.T, axis=0, keepdims=True))
-    left = left_ref[:, 16:48, :].reshape(1024, 128)
+    left = jnp.concatenate([left_ref[:, 4:11], left_ref[:, 10:11]], axis=1).astype(F32)
+    left = left.reshape(1024, 128).astype(BF16)
+    upper = iota((8, 128), 0) < 4
     tails = []
     for l in range(4):
         pltpu.make_async_copy(outer_hbm.at[l], outer_ref.at[l], sems.at[8 - EARLY + l]).wait()
@@ -148,7 +148,8 @@
         total = jnp.zeros((8, 128), F32)
         for c in range(32):
             here = slice(56 * c, 56 * c + 56)
-            two = jnp.concatenate([delta[32 * c : 32 * c + 32, 0:128], delta[32 * c : 32 * c + 24, 128:256]], axis=0)
+            a, b = delta[32 * c : 32 * c + 32, 0:128], delta[32 * c : 32 * c + 32, 128:256]
+            two = jnp.concatenate([a[0:24], b[0:24], jnp.where(upper, a[24:32], b[24:32])], axis=0)
             full = outer_ref[l, here, :].astype(F32) + two
             outer_full_ref[l, here, :] = full
             total += jnp.sum((full * full).reshape(7, 8, 128), axis=0)
@@ -208,7 +209,7 @@
     outer_base = outer_base.reshape(4, 1792, 128)
     left, right = pl.pallas_call(
         pack_kernel,
-        out_shape=(jax.ShapeDtypeStruct((cols, 48, 128), BF16), pltpu.VMEM((16, 512), BF16)),
+        out_shape=(jax.ShapeDtypeStruct((cols, 11, 4, 128), BF16), pltpu.VMEM((16, 512), BF16)),
         in_specs=[in_hbm()] * 4,
         out_specs=(in_hbm(), whole()),
         scratch_shapes=[
@@ -216,7 +217,7 @@
             pltpu.VMEM((4, 16, 56), BF16),
             pltpu.VMEM((8, 2, 448), BF16),
             pltpu.VMEM((4, 2, 128), BF16),
-            pltpu.VMEM((cols, 48, 128), BF16),
+            pltpu.VMEM((cols, 11, 4, 128), BF16),
             pltpu.SemaphoreType.DMA((5,)),
         ],
         compiler_params=params(4),

time: 43.9 us -> 43.4 us (0.989)
  waiting for transfers between devices: 9.1 us -> 8.33 us
    all_to_all x1, waiting for transfers between devices: 1.66 us -> 0.91 us  [shards(): left = lax.all_to_all(left, 'col', 0, 0, tiled=True)]
  transfers between devices with their start and end apart: 9 -> 9, of which waited for: 6 -> 6; matrix products, arithmetic and copies ran while one was open for 0% -> 0% of each run, Pallas kernels for 4% -> 5%
where the time goes in v4:
time: 43.4 us; the launch traced here: 43.1 us
  starting transfers between devices  25 us (58%)
  Pallas kernels  9.13 us (21%)
  waiting for transfers between devices  8.33 us (19%)
  between operations  0.69 us (2%)
    ppermute x8, starting transfers between devices, swapped(): lax.ppermute(value, 'row', [(i, i ^ d) for i in range(lax.axis_size('row'...  13.1 us
    all_to_all x1, starting transfers between devices, shards(): left = lax.all_to_all(left, 'col', 0, 0, tiled=True)  11.9 us
    ppermute x8, waiting for transfers between devices, swapped(): lax.ppermute(value, 'row', [(i, i ^ d) for i in range(lax.axis_size('row'...  7.42 us
    pallas_call x1, Pallas kernels, shards(): pl.pallas_call(scale_kernel, out_shape=(jax.ShapeDtypeStruct((8, 448, 512...  2.73 us
    pallas_call x1, Pallas kernels, shards(): pl.pallas_call(squares_kernel, out_shape=(pltpu.VMEM((8, 448, 512), F32),...  2.61 us
    pallas_call x1, Pallas kernels, shards(): pl.pallas_call(pack_kernel, out_shape=(jax.ShapeDtypeStruct((cols, 11, 4,...  1.83 us
    pallas_call x1, Pallas kernels, shards(): pl.pallas_call(load_kernel, out_shape=pltpu.VMEM((EARLY, 448, 512), BF16)...  1.79 us
    all_to_all x1, waiting for transfers between devices, shards(): left = lax.all_to_all(left, 'col', 0, 0, tiled=True)  0.91 us
  transfers between devices with their start and end apart: 9, of which 6 were waited for; matrix products, arithmetic and copies ran while one was open for 0% of the time, Pallas kernels for 5%

profile of v4, /device:TPU:1, one launch (start us, length us, event | category | flops | bytes accessed | tf_op | source)
XLA Modules:
  0.0 43.1 jit_solution(6381243558423860411)
XLA Ops:
  0.6 1.8 %pack.1 = (bf16[32,11,4,128]{3,2,1,0:T(4,128)(2,1)}, bf16[16,512]{1,0:T(8,128)(2,1)S(1)}) custom-call(bf16[8,16,16]{2,1,0:T(8,128)(2,1)} %bitcast.28, bf16[4,16,56]{2,1,0:T(8,128)(2,1)} %bitcast.29, bf16[8,2,448]{2,1,0:T(2,128)(2,1)} %bitcast.30, bf16[4,2,128]{2,1,0:T(2,128)(2,1)} %bitcast.32), custom_call_target="tpu_custom_call" | custom-call | tf_op jit(solution)/shard_map/pack/pallas_call | solution.py:210
  2.5 11.9 %all-to-all-start = ((bf16[32,11,4,128]{3,2,1,0:T(4,128)(2,1)}), bf16[32,11,4,128]{3,2,1,0:T(4,128)(2,1)S(1)}, u32[]{:S(2)}, u32[]{:S(2)}) async-start(bf16[32,11,4,128]{3,2,1,0:T(4,128)(2,1)} %get-tuple-element.11), calls=%async_computation | async-start | bytes 720896 | tf_op jit(solution)/shard_map/all_to_all | solution.py:232
  14.3 1.0 %collective-permute-start = (bf16[16,512]{1,0:T(8,128)(2,1)S(1)}, bf16[16,512]{1,0:T(8,128)(2,1)S(1)}, u32[]{:S(2)}, u32[]{:S(2)}) collective-permute-start(bf16[16,512]{1,0:T(8,128)(2,1)S(1)} %get-tuple-element.12), channel_id=1, source_target_pairs={{0,32},{32,0},{64,96},{96,64},{128,160},{160,128},{192,224},{224,1... | collective-permute-start | bytes 49160 | tf_op jit(solution)/shard_map/ppermute | solution.py:201
  15.4 0.8 %collective-permute-done = bf16[16,512]{1,0:T(8,128)(2,1)S(1)} collective-permute-done((bf16[16,512]{1,0:T(8,128)(2,1)S(1)}, bf16[16,512]{1,0:T(8,128)(2,1)S(1)}, u32[]{:S(2)}, u32[]{:S(2)}) %collective-permute-start) | collective-permute-done | bytes 16416 | tf_op jit(solution)/shard_map/ppermute | solution.py:201
  16.2 3.1 %collective-permute-start.3 = (bf16[2,16,512]{2,1,0:T(8,128)(2,1)S(1)}, bf16[2,16,512]{2,1,0:T(8,128)(2,1)S(1)}, u32[]{:S(2)}, u32[]{:S(2)}) collective-permute-start(bf16[2,16,512]{2,1,0:T(8,128)(2,1)S(1)} %pad_maximum_fusion.own_ref), channel_id=1, source_target_pairs={{0,160},{32,128},{64,224},{96,192},{128,32},{160,0},{192,96},{224,... | collective-permute-start | bytes 98312 | tf_op jit(solution)/shard_map/ppermute | solution.py:201
  19.4 0.8 %collective-permute-start.2 = (bf16[2,16,512]{2,1,0:T(8,128)(2,1)S(1)}, bf16[2,16,512]{2,1,0:T(8,128)(2,1)S(1)}, u32[]{:S(2)}, u32[]{:S(2)}) collective-permute-start(bf16[2,16,512]{2,1,0:T(8,128)(2,1)S(1)} %pad_maximum_fusion.own_ref), channel_id=1, source_target_pairs={{0,224},{32,192},{64,160},{96,128},{128,96},{160,64},{192,32},{224... | collective-permute-start | bytes 98312 | tf_op jit(solution)/shard_map/ppermute | solution.py:201
  20.2 0.0 collective-permute-start.1
  20.2 1.8 %load.1.early_ref = bf16[6,448,512]{2,1,0:T(8,128)(2,1)S(1)} custom-call(bf16[8,448,512]{2,1,0:T(8,128)(2,1)} %bitcast.25), custom_call_target="tpu_custom_call" | custom-call | tf_op jit(solution)/shard_map/load/pallas_call | solution.py:235
  22.0 0.0 collective-permute-done.3.three_ref
  22.0 2.2 %collective-permute-done.2.two_ref = bf16[2,16,512]{2,1,0:T(8,128)(2,1)S(1)} collective-permute-done((bf16[2,16,512]{2,1,0:T(8,128)(2,1)S(1)}, bf16[2,16,512]{2,1,0:T(8,128)(2,1)S(1)}, u32[]{:S(2)}, u32[]{:S(2)}) %collective-permute-start.2) | collective-permute-done | bytes 32800 | tf_op jit(solution)/shard_map/ppermute | solution.py:201
  24.2 0.0 collective-permute-done.1.one_ref
  24.2 0.2 gather_right.1
  24.4 0.9 %all-to-all-done.left_ref = bf16[32,11,4,128]{3,2,1,0:T(4,128)(2,1)S(1)} async-done(((bf16[32,11,4,128]{3,2,1,0:T(4,128)(2,1)}), bf16[32,11,4,128]{3,2,1,0:T(4,128)(2,1)S(1)}, u32[]{:S(2)}, u32[]{:S(2)}) %all-to-all-start) | async-done | bytes 360480 | tf_op jit(solution)/shard_map/all_to_all | solution.py:232
  25.3 0.0 copy-start
  25.3 0.0 copy-start.1
  25.3 2.6 %squares.1 = (f32[8,448,512]{2,1,0:T(8,128)S(1)}, f32[4,1792,128]{2,1,0:T(8,128)S(1)}, f32[8,512]{1,0:T(8,128)S(1)}) custom-call(bf16[32,11,4,128]{3,2,1,0:T(4,128)(2,1)S(1)} %all-to-all-done.left_ref, bf16[448,128]{1,0:T(8,128)(2,1)S(1)} %get-tuple-element.13.inner_right_ref, bf16[4,128,256]{2,1,0:T(8,128)(2,1)S(1)} %get-tuple-element.14.outer_right_ref, ...), custom_call_target="tpu_custom_call" | custom-call | tf_op jit(solution)/shard_map/squares/pallas_call | solution.py:253
  27.9 4.1 %collective-permute-start.4 = (f32[8,512]{1,0:T(8,128)S(1)}, f32[8,512]{1,0:T(8,128)S(1)}, u32[]{:S(2)}, u32[]{:S(2)}) collective-permute-start(f32[8,512]{1,0:T(8,128)S(1)} %get-tuple-element.15), channel_id=1, source_target_pairs={{0,32},{32,0},{64,96},{96,64},{128,160},{160,128},{192,224},{224,1... | collective-permute-start | bytes 49160 | tf_op jit(solution)/shard_map/ppermute | solution.py:201
  32.0 0.8 %collective-permute-done.4 = f32[8,512]{1,0:T(8,128)S(1)} collective-permute-done((f32[8,512]{1,0:T(8,128)S(1)}, f32[8,512]{1,0:T(8,128)S(1)}, u32[]{:S(2)}, u32[]{:S(2)}) %collective-permute-start.4) | collective-permute-done | bytes 16416 | tf_op jit(solution)/shard_map/ppermute | solution.py:201
  32.9 3.1 %collective-permute-start.7 = (f32[8,512]{1,0:T(8,128)S(1)}, f32[8,512]{1,0:T(8,128)S(1)}, u32[]{:S(2)}, u32[]{:S(2)}) collective-permute-start(f32[8,512]{1,0:T(8,128)S(1)} %add.3.own_ref), channel_id=1, source_target_pairs={{0,160},{32,128},{64,224},{96,192},{128,32},{160,0},{192,96},{224,... | collective-permute-start | bytes 49160 | tf_op jit(solution)/shard_map/ppermute | solution.py:201
  36.0 0.8 %collective-permute-start.6 = (f32[8,512]{1,0:T(8,128)S(1)}, f32[8,512]{1,0:T(8,128)S(1)}, u32[]{:S(2)}, u32[]{:S(2)}) collective-permute-start(f32[8,512]{1,0:T(8,128)S(1)} %add.3.own_ref), channel_id=1, source_target_pairs={{0,224},{32,192},{64,160},{96,128},{128,96},{160,64},{192,32},{224... | collective-permute-start | bytes 49160 | tf_op jit(solution)/shard_map/ppermute | solution.py:201
  36.9 0.0 collective-permute-start.5
  36.9 0.7 %collective-permute-done.7.three_ref = f32[8,512]{1,0:T(8,128)S(1)} collective-permute-done((f32[8,512]{1,0:T(8,128)S(1)}, f32[8,512]{1,0:T(8,128)S(1)}, u32[]{:S(2)}, u32[]{:S(2)}) %collective-permute-start.7) | collective-permute-done | bytes 16416 | tf_op jit(solution)/shard_map/ppermute | solution.py:201
  37.6 2.9 %collective-permute-done.6.two_ref = f32[8,512]{1,0:T(8,128)S(1)} collective-permute-done((f32[8,512]{1,0:T(8,128)S(1)}, f32[8,512]{1,0:T(8,128)S(1)}, u32[]{:S(2)}, u32[]{:S(2)}) %collective-permute-start.6) | collective-permute-done | bytes 16416 | tf_op jit(solution)/shard_map/ppermute | solution.py:201
  40.4 0.0 collective-permute-done.5.one_ref
  40.4 0.0 copy-done
  40.4 0.0 copy-done.1
  40.4 2.7 %scale.1 = (bf16[8,448,512]{2,1,0:T(8,128)(2,1)}, bf16[4,1792,128]{2,1,0:T(8,128)(2,1)}) custom-call(f32[8,512]{1,0:T(8,128)S(1)} %add.3.own_ref, f32[8,512]{1,0:T(8,128)S(1)} %collective-permute-done.5.one_ref, f32[8,512]{1,0:T(8,128)S(1)} %collective-permute-done.6.two_ref, f32[8,512]{1,0:T(8,128)S(1)} %collective-permute-done.7.three_ref, ...), custom_call_target="tpu_custom_call" | custom-call | tf_op jit(solution)/shard_map/scale/pallas_call | solution.py:272
  (2 shorter events, 0.0 us)
Async XLA Ops:
  2.5 22.8 %all-to-all-start = ((bf16[32,11,4,128]{3,2,1,0:T(4,128)(2,1)}), bf16[32,11,4,128]{3,2,1,0:T(4,128)(2,1)S(1)}, u32[]{:S(2)}, u32[]{:S(2)}) async-start(bf16[32,11,4,128]{3,2,1,0:T(4,128)(2,1)} %get-tuple-element.11), calls=%async_computation | async-start | bytes 720896 | tf_op jit(solution)/shard_map/all_to_all | solution.py:232
  14.3 1.9 %collective-permute-start = (bf16[16,512]{1,0:T(8,128)(2,1)S(1)}, bf16[16,512]{1,0:T(8,128)(2,1)S(1)}, u32[]{:S(2)}, u32[]{:S(2)}) collective-permute-start(bf16[16,512]{1,0:T(8,128)(2,1)S(1)} %get-tuple-element.12), channel_id=1, source_target_pairs={{0,32},{32,0},{64,96},{96,64},{128,160},{160,128},{192,224},{224,1... | collective-permute-start | bytes 49160 | tf_op jit(solution)/shard_map/ppermute | solution.py:201
  16.2 5.8 %collective-permute-start.3 = (bf16[2,16,512]{2,1,0:T(8,128)(2,1)S(1)}, bf16[2,16,512]{2,1,0:T(8,128)(2,1)S(1)}, u32[]{:S(2)}, u32[]{:S(2)}) collective-permute-start(bf16[2,16,512]{2,1,0:T(8,128)(2,1)S(1)} %pad_maximum_fusion.own_ref), channel_id=1, source_target_pairs={{0,160},{32,128},{64,224},{96,192},{128,32},{160,0},{192,96},{224,... | collective-permute-start | bytes 98312 | tf_op jit(solution)/shard_map/ppermute | solution.py:201
  19.4 4.8 %collective-permute-start.2 = (bf16[2,16,512]{2,1,0:T(8,128)(2,1)S(1)}, bf16[2,16,512]{2,1,0:T(8,128)(2,1)S(1)}, u32[]{:S(2)}, u32[]{:S(2)}) collective-permute-start(bf16[2,16,512]{2,1,0:T(8,128)(2,1)S(1)} %pad_maximum_fusion.own_ref), channel_id=1, source_target_pairs={{0,224},{32,192},{64,160},{96,128},{128,96},{160,64},{192,32},{224... | collective-permute-start | bytes 98312 | tf_op jit(solution)/shard_map/ppermute | solution.py:201
  20.2 4.0 %collective-permute-start.1 = (bf16[2,16,512]{2,1,0:T(8,128)(2,1)S(1)}, bf16[2,16,512]{2,1,0:T(8,128)(2,1)S(1)}, u32[]{:S(2)}, u32[]{:S(2)}) collective-permute-start(bf16[2,16,512]{2,1,0:T(8,128)(2,1)S(1)} %pad_maximum_fusion.own_ref), channel_id=1, source_target_pairs={{0,96},{32,64},{64,32},{96,0},{128,224},{160,192},{192,160},{224,1... | collective-permute-start | bytes 98312 | tf_op jit(solution)/shard_map/ppermute | solution.py:201
  25.3 15.1 %copy-start = (f32[4,1,2,448]{3,2,1,0:T(2,128)S(1)}, f32[4,1,2,448]{3,2,1,0:T(2,128)}, u32[]{:S(2)}) copy-start(f32[4,1,2,448]{3,2,1,0:T(2,128)} %param.11) | copy-start | bytes 43012
  25.3 15.1 %copy-start.1 = (f32[4,1,128]{2,1,0:T(1,128)S(1)}, f32[4,1,128]{2,1,0:T(1,128)}, u32[]{:S(2)}) copy-start(f32[4,1,128]{2,1,0:T(1,128)} %outer_mag_ref.1) | copy-start | bytes 6148
  27.9 5.0 %collective-permute-start.4 = (f32[8,512]{1,0:T(8,128)S(1)}, f32[8,512]{1,0:T(8,128)S(1)}, u32[]{:S(2)}, u32[]{:S(2)}) collective-permute-start(f32[8,512]{1,0:T(8,128)S(1)} %get-tuple-element.15), channel_id=1, source_target_pairs={{0,32},{32,0},{64,96},{96,64},{128,160},{160,128},{192,224},{224,1... | collective-permute-start | bytes 49160 | tf_op jit(solution)/shard_map/ppermute | solution.py:201
  32.9 4.7 %collective-permute-start.7 = (f32[8,512]{1,0:T(8,128)S(1)}, f32[8,512]{1,0:T(8,128)S(1)}, u32[]{:S(2)}, u32[]{:S(2)}) collective-permute-start(f32[8,512]{1,0:T(8,128)S(1)} %add.3.own_ref), channel_id=1, source_target_pairs={{0,160},{32,128},{64,224},{96,192},{128,32},{160,0},{192,96},{224,... | collective-permute-start | bytes 49160 | tf_op jit(solution)/shard_map/ppermute | solution.py:201
  36.0 4.4 %collective-permute-start.6 = (f32[8,512]{1,0:T(8,128)S(1)}, f32[8,512]{1,0:T(8,128)S(1)}, u32[]{:S(2)}, u32[]{:S(2)}) collective-permute-start(f32[8,512]{1,0:T(8,128)S(1)} %add.3.own_ref), channel_id=1, source_target_pairs={{0,224},{32,192},{64,160},{96,128},{128,96},{160,64},{192,32},{224... | collective-permute-start | bytes 49160 | tf_op jit(solution)/shard_map/ppermute | solution.py:201
  36.9 3.6 %collective-permute-start.5 = (f32[8,512]{1,0:T(8,128)S(1)}, f32[8,512]{1,0:T(8,128)S(1)}, u32[]{:S(2)}, u32[]{:S(2)}) collective-permute-start(f32[8,512]{1,0:T(8,128)S(1)} %add.3.own_ref), channel_id=1, source_target_pairs={{0,96},{32,64},{64,32},{96,0},{128,224},{160,192},{192,160},{224,1... | collective-permute-start | bytes 49160 | tf_op jit(solution)/shard_map/ppermute | solution.py:201

commit v5 on v4

--- a/solution.py
+++ b/solution.py
@@ -49,15 +49,17 @@
     inner_left_hbm, outer_left_hbm, inner_right_hbm, outer_right_hbm, left_out, right_out,
     inner_left_ref, outer_left_ref, inner_right_ref, outer_right_ref, left_ref, sems
 ):
-    fetch(
-        [
-            (inner_left_hbm, inner_left_ref),
-            (outer_left_hbm, outer_left_ref),
-            (inner_right_hbm, inner_right_ref),
-            (outer_right_hbm, outer_right_ref),
-        ],
-        sems,
-    )
+    pairs = [
+        (inner_left_hbm, inner_left_ref),
+        (outer_left_hbm, outer_left_ref),
+        (inner_right_hbm, inner_right_ref),
+        (outer_right_hbm, outer_right_ref),
+    ]
+    copies = [pltpu.make_async_copy(a, b, sems.at[i]) for i, (a, b) in enumerate(pairs)]
+    for copy in copies:
+        copy.start()
+    for copy in copies[:2]:
+        copy.wait()
     k, lane = iota((16, 128), 0), iota((16, 128), 1)
     inner = jnp.zeros((16, 128), F32)
     for m in range(8):
@@ -75,6 +77,8 @@
         left_ref[i] = block.reshape(11, 4, 128).astype(BF16)
     sent = pltpu.make_async_copy(left_ref, left_out, sems.at[4])
     sent.start()
+    for copy in copies[2:]:
+        copy.wait()
     row, e = iota((16, 2), 0), iota((16, 2), 1)
     inner = jnp.zeros((16, 448), F32)
     for m in range(8):

time: 43.4 us -> 43.4 us (level)
  no operation moved by 1% of the time
where the time goes in v5:
time: 43.4 us; the launch traced here: 43.1 us
  starting transfers between devices  25 us (58%)
  Pallas kernels  9.12 us (21%)
  waiting for transfers between devices  8.33 us (19%)
  between operations  0.69 us (2%)
    ppermute x8, starting transfers between devices, swapped(): lax.ppermute(value, 'row', [(i, i ^ d) for i in range(lax.axis_size('row'...  13.1 us
    all_to_all x1, starting transfers between devices, shards(): left = lax.all_to_all(left, 'col', 0, 0, tiled=True)  11.9 us
    ppermute x8, waiting for transfers between devices, swapped(): lax.ppermute(value, 'row', [(i, i ^ d) for i in range(lax.axis_size('row'...  7.42 us
    pallas_call x1, Pallas kernels, shards(): pl.pallas_call(scale_kernel, out_shape=(jax.ShapeDtypeStruct((8, 448, 512...  2.73 us
    pallas_call x1, Pallas kernels, shards(): pl.pallas_call(squares_kernel, out_shape=(pltpu.VMEM((8, 448, 512), F32),...  2.61 us
    pallas_call x1, Pallas kernels, shards(): pl.pallas_call(pack_kernel, out_shape=(jax.ShapeDtypeStruct((cols, 11, 4,...  1.82 us
    pallas_call x1, Pallas kernels, shards(): pl.pallas_call(load_kernel, out_shape=pltpu.VMEM((EARLY, 448, 512), BF16)...  1.79 us
    all_to_all x1, waiting for transfers between devices, shards(): left = lax.all_to_all(left, 'col', 0, 0, tiled=True)  0.91 us
  transfers between devices with their start and end apart: 9, of which 6 were waited for; matrix products, arithmetic and copies ran while one was open for 0% of the time, Pallas kernels for 5%

profile of v5, /device:TPU:1, one launch (start us, length us, event | category | flops | bytes accessed | tf_op | source)
XLA Modules:
  0.0 43.1 jit_solution(3955780948264176799)
XLA Ops:
  0.6 1.8 %pack.1 = (bf16[32,11,4,128]{3,2,1,0:T(4,128)(2,1)}, bf16[16,512]{1,0:T(8,128)(2,1)S(1)}) custom-call(bf16[8,16,16]{2,1,0:T(8,128)(2,1)} %bitcast.28, bf16[4,16,56]{2,1,0:T(8,128)(2,1)} %bitcast.29, bf16[8,2,448]{2,1,0:T(2,128)(2,1)} %bitcast.30, bf16[4,2,128]{2,1,0:T(2,128)(2,1)} %bitcast.32), custom_call_target="tpu_custom_call" | custom-call | tf_op jit(solution)/shard_map/pack/pallas_call | solution.py:214
  2.5 11.9 %all-to-all-start = ((bf16[32,11,4,128]{3,2,1,0:T(4,128)(2,1)}), bf16[32,11,4,128]{3,2,1,0:T(4,128)(2,1)S(1)}, u32[]{:S(2)}, u32[]{:S(2)}) async-start(bf16[32,11,4,128]{3,2,1,0:T(4,128)(2,1)} %get-tuple-element.11), calls=%async_computation | async-start | bytes 720896 | tf_op jit(solution)/shard_map/all_to_all | solution.py:236
  14.3 1.0 %collective-permute-start = (bf16[16,512]{1,0:T(8,128)(2,1)S(1)}, bf16[16,512]{1,0:T(8,128)(2,1)S(1)}, u32[]{:S(2)}, u32[]{:S(2)}) collective-permute-start(bf16[16,512]{1,0:T(8,128)(2,1)S(1)} %get-tuple-element.12), channel_id=1, source_target_pairs={{0,32},{32,0},{64,96},{96,64},{128,160},{160,128},{192,224},{224,1... | collective-permute-start | bytes 49160 | tf_op jit(solution)/shard_map/ppermute | solution.py:205
  15.4 0.8 %collective-permute-done = bf16[16,512]{1,0:T(8,128)(2,1)S(1)} collective-permute-done((bf16[16,512]{1,0:T(8,128)(2,1)S(1)}, bf16[16,512]{1,0:T(8,128)(2,1)S(1)}, u32[]{:S(2)}, u32[]{:S(2)}) %collective-permute-start) | collective-permute-done | bytes 16416 | tf_op jit(solution)/shard_map/ppermute | solution.py:205
  16.2 3.1 %collective-permute-start.3 = (bf16[2,16,512]{2,1,0:T(8,128)(2,1)S(1)}, bf16[2,16,512]{2,1,0:T(8,128)(2,1)S(1)}, u32[]{:S(2)}, u32[]{:S(2)}) collective-permute-start(bf16[2,16,512]{2,1,0:T(8,128)(2,1)S(1)} %pad_maximum_fusion.own_ref), channel_id=1, source_target_pairs={{0,160},{32,128},{64,224},{96,192},{128,32},{160,0},{192,96},{224,... | collective-permute-start | bytes 98312 | tf_op jit(solution)/shard_map/ppermute | solution.py:205
  19.4 0.8 %collective-permute-start.2 = (bf16[2,16,512]{2,1,0:T(8,128)(2,1)S(1)}, bf16[2,16,512]{2,1,0:T(8,128)(2,1)S(1)}, u32[]{:S(2)}, u32[]{:S(2)}) collective-permute-start(bf16[2,16,512]{2,1,0:T(8,128)(2,1)S(1)} %pad_maximum_fusion.own_ref), channel_id=1, source_target_pairs={{0,224},{32,192},{64,160},{96,128},{128,96},{160,64},{192,32},{224... | collective-permute-start | bytes 98312 | tf_op jit(solution)/shard_map/ppermute | solution.py:205
  20.2 0.0 collective-permute-start.1
  20.2 1.8 %load.1.early_ref = bf16[6,448,512]{2,1,0:T(8,128)(2,1)S(1)} custom-call(bf16[8,448,512]{2,1,0:T(8,128)(2,1)} %bitcast.25), custom_call_target="tpu_custom_call" | custom-call | tf_op jit(solution)/shard_map/load/pallas_call | solution.py:239
  22.0 0.0 collective-permute-done.3.three_ref
  22.0 2.2 %collective-permute-done.2.two_ref = bf16[2,16,512]{2,1,0:T(8,128)(2,1)S(1)} collective-permute-done((bf16[2,16,512]{2,1,0:T(8,128)(2,1)S(1)}, bf16[2,16,512]{2,1,0:T(8,128)(2,1)S(1)}, u32[]{:S(2)}, u32[]{:S(2)}) %collective-permute-start.2) | collective-permute-done | bytes 32800 | tf_op jit(solution)/shard_map/ppermute | solution.py:205
  24.2 0.0 collective-permute-done.1.one_ref
  24.2 0.2 gather_right.1
  24.4 0.9 %all-to-all-done.left_ref = bf16[32,11,4,128]{3,2,1,0:T(4,128)(2,1)S(1)} async-done(((bf16[32,11,4,128]{3,2,1,0:T(4,128)(2,1)}), bf16[32,11,4,128]{3,2,1,0:T(4,128)(2,1)S(1)}, u32[]{:S(2)}, u32[]{:S(2)}) %all-to-all-start) | async-done | bytes 360480 | tf_op jit(solution)/shard_map/all_to_all | solution.py:236
  25.3 0.0 copy-start
  25.3 0.0 copy-start.1
  25.3 2.6 %squares.1 = (f32[8,448,512]{2,1,0:T(8,128)S(1)}, f32[4,1792,128]{2,1,0:T(8,128)S(1)}, f32[8,512]{1,0:T(8,128)S(1)}) custom-call(bf16[32,11,4,128]{3,2,1,0:T(4,128)(2,1)S(1)} %all-to-all-done.left_ref, bf16[448,128]{1,0:T(8,128)(2,1)S(1)} %get-tuple-element.13.inner_right_ref, bf16[4,128,256]{2,1,0:T(8,128)(2,1)S(1)} %get-tuple-element.14.outer_right_ref, ...), custom_call_target="tpu_custom_call" | custom-call | tf_op jit(solution)/shard_map/squares/pallas_call | solution.py:257
  27.9 4.1 %collective-permute-start.4 = (f32[8,512]{1,0:T(8,128)S(1)}, f32[8,512]{1,0:T(8,128)S(1)}, u32[]{:S(2)}, u32[]{:S(2)}) collective-permute-start(f32[8,512]{1,0:T(8,128)S(1)} %get-tuple-element.15), channel_id=1, source_target_pairs={{0,32},{32,0},{64,96},{96,64},{128,160},{160,128},{192,224},{224,1... | collective-permute-start | bytes 49160 | tf_op jit(solution)/shard_map/ppermute | solution.py:205
  32.0 0.8 %collective-permute-done.4 = f32[8,512]{1,0:T(8,128)S(1)} collective-permute-done((f32[8,512]{1,0:T(8,128)S(1)}, f32[8,512]{1,0:T(8,128)S(1)}, u32[]{:S(2)}, u32[]{:S(2)}) %collective-permute-start.4) | collective-permute-done | bytes 16416 | tf_op jit(solution)/shard_map/ppermute | solution.py:205
  32.9 3.1 %collective-permute-start.7 = (f32[8,512]{1,0:T(8,128)S(1)}, f32[8,512]{1,0:T(8,128)S(1)}, u32[]{:S(2)}, u32[]{:S(2)}) collective-permute-start(f32[8,512]{1,0:T(8,128)S(1)} %add.3.own_ref), channel_id=1, source_target_pairs={{0,160},{32,128},{64,224},{96,192},{128,32},{160,0},{192,96},{224,... | collective-permute-start | bytes 49160 | tf_op jit(solution)/shard_map/ppermute | solution.py:205
  36.0 0.8 %collective-permute-start.6 = (f32[8,512]{1,0:T(8,128)S(1)}, f32[8,512]{1,0:T(8,128)S(1)}, u32[]{:S(2)}, u32[]{:S(2)}) collective-permute-start(f32[8,512]{1,0:T(8,128)S(1)} %add.3.own_ref), channel_id=1, source_target_pairs={{0,224},{32,192},{64,160},{96,128},{128,96},{160,64},{192,32},{224... | collective-permute-start | bytes 49160 | tf_op jit(solution)/shard_map/ppermute | solution.py:205
  36.8 0.0 collective-permute-start.5
  36.8 0.7 %collective-permute-done.7.three_ref = f32[8,512]{1,0:T(8,128)S(1)} collective-permute-done((f32[8,512]{1,0:T(8,128)S(1)}, f32[8,512]{1,0:T(8,128)S(1)}, u32[]{:S(2)}, u32[]{:S(2)}) %collective-permute-start.7) | collective-permute-done | bytes 16416 | tf_op jit(solution)/shard_map/ppermute | solution.py:205
  37.5 2.9 %collective-permute-done.6.two_ref = f32[8,512]{1,0:T(8,128)S(1)} collective-permute-done((f32[8,512]{1,0:T(8,128)S(1)}, f32[8,512]{1,0:T(8,128)S(1)}, u32[]{:S(2)}, u32[]{:S(2)}) %collective-permute-start.6) | collective-permute-done | bytes 16416 | tf_op jit(solution)/shard_map/ppermute | solution.py:205
  40.4 0.0 collective-permute-done.5.one_ref
  40.4 0.0 copy-done
  40.4 0.0 copy-done.1
  40.4 2.7 %scale.1 = (bf16[8,448,512]{2,1,0:T(8,128)(2,1)}, bf16[4,1792,128]{2,1,0:T(8,128)(2,1)}) custom-call(f32[8,512]{1,0:T(8,128)S(1)} %add.3.own_ref, f32[8,512]{1,0:T(8,128)S(1)} %collective-permute-done.5.one_ref, f32[8,512]{1,0:T(8,128)S(1)} %collective-permute-done.6.two_ref, f32[8,512]{1,0:T(8,128)S(1)} %collective-permute-done.7.three_ref, ...), custom_call_target="tpu_custom_call" | custom-call | tf_op jit(solution)/shard_map/scale/pallas_call | solution.py:276
  (2 shorter events, 0.0 us)
Async XLA Ops:
  2.5 22.8 %all-to-all-start = ((bf16[32,11,4,128]{3,2,1,0:T(4,128)(2,1)}), bf16[32,11,4,128]{3,2,1,0:T(4,128)(2,1)S(1)}, u32[]{:S(2)}, u32[]{:S(2)}) async-start(bf16[32,11,4,128]{3,2,1,0:T(4,128)(2,1)} %get-tuple-element.11), calls=%async_computation | async-start | bytes 720896 | tf_op jit(solution)/shard_map/all_to_all | solution.py:236
  14.3 1.9 %collective-permute-start = (bf16[16,512]{1,0:T(8,128)(2,1)S(1)}, bf16[16,512]{1,0:T(8,128)(2,1)S(1)}, u32[]{:S(2)}, u32[]{:S(2)}) collective-permute-start(bf16[16,512]{1,0:T(8,128)(2,1)S(1)} %get-tuple-element.12), channel_id=1, source_target_pairs={{0,32},{32,0},{64,96},{96,64},{128,160},{160,128},{192,224},{224,1... | collective-permute-start | bytes 49160 | tf_op jit(solution)/shard_map/ppermute | solution.py:205
  16.2 5.8 %collective-permute-start.3 = (bf16[2,16,512]{2,1,0:T(8,128)(2,1)S(1)}, bf16[2,16,512]{2,1,0:T(8,128)(2,1)S(1)}, u32[]{:S(2)}, u32[]{:S(2)}) collective-permute-start(bf16[2,16,512]{2,1,0:T(8,128)(2,1)S(1)} %pad_maximum_fusion.own_ref), channel_id=1, source_target_pairs={{0,160},{32,128},{64,224},{96,192},{128,32},{160,0},{192,96},{224,... | collective-permute-start | bytes 98312 | tf_op jit(solution)/shard_map/ppermute | solution.py:205
  19.4 4.8 %collective-permute-start.2 = (bf16[2,16,512]{2,1,0:T(8,128)(2,1)S(1)}, bf16[2,16,512]{2,1,0:T(8,128)(2,1)S(1)}, u32[]{:S(2)}, u32[]{:S(2)}) collective-permute-start(bf16[2,16,512]{2,1,0:T(8,128)(2,1)S(1)} %pad_maximum_fusion.own_ref), channel_id=1, source_target_pairs={{0,224},{32,192},{64,160},{96,128},{128,96},{160,64},{192,32},{224... | collective-permute-start | bytes 98312 | tf_op jit(solution)/shard_map/ppermute | solution.py:205
  20.2 4.0 %collective-permute-start.1 = (bf16[2,16,512]{2,1,0:T(8,128)(2,1)S(1)}, bf16[2,16,512]{2,1,0:T(8,128)(2,1)S(1)}, u32[]{:S(2)}, u32[]{:S(2)}) collective-permute-start(bf16[2,16,512]{2,1,0:T(8,128)(2,1)S(1)} %pad_maximum_fusion.own_ref), channel_id=1, source_target_pairs={{0,96},{32,64},{64,32},{96,0},{128,224},{160,192},{192,160},{224,1... | collective-permute-start | bytes 98312 | tf_op jit(solution)/shard_map/ppermute | solution.py:205
  25.3 15.1 %copy-start = (f32[4,1,2,448]{3,2,1,0:T(2,128)S(1)}, f32[4,1,2,448]{3,2,1,0:T(2,128)}, u32[]{:S(2)}) copy-start(f32[4,1,2,448]{3,2,1,0:T(2,128)} %param.11) | copy-start | bytes 43012
  25.3 15.1 %copy-start.1 = (f32[4,1,128]{2,1,0:T(1,128)S(1)}, f32[4,1,128]{2,1,0:T(1,128)}, u32[]{:S(2)}) copy-start(f32[4,1,128]{2,1,0:T(1,128)} %outer_mag_ref.1) | copy-start | bytes 6148
  27.9 5.0 %collective-permute-start.4 = (f32[8,512]{1,0:T(8,128)S(1)}, f32[8,512]{1,0:T(8,128)S(1)}, u32[]{:S(2)}, u32[]{:S(2)}) collective-permute-start(f32[8,512]{1,0:T(8,128)S(1)} %get-tuple-element.15), channel_id=1, source_target_pairs={{0,32},{32,0},{64,96},{96,64},{128,160},{160,128},{192,224},{224,1... | collective-permute-start | bytes 49160 | tf_op jit(solution)/shard_map/ppermute | solution.py:205
  32.9 4.7 %collective-permute-start.7 = (f32[8,512]{1,0:T(8,128)S(1)}, f32[8,512]{1,0:T(8,128)S(1)}, u32[]{:S(2)}, u32[]{:S(2)}) collective-permute-start(f32[8,512]{1,0:T(8,128)S(1)} %add.3.own_ref), channel_id=1, source_target_pairs={{0,160},{32,128},{64,224},{96,192},{128,32},{160,0},{192,96},{224,... | collective-permute-start | bytes 49160 | tf_op jit(solution)/shard_map/ppermute | solution.py:205
  36.0 4.4 %collective-permute-start.6 = (f32[8,512]{1,0:T(8,128)S(1)}, f32[8,512]{1,0:T(8,128)S(1)}, u32[]{:S(2)}, u32[]{:S(2)}) collective-permute-start(f32[8,512]{1,0:T(8,128)S(1)} %add.3.own_ref), channel_id=1, source_target_pairs={{0,224},{32,192},{64,160},{96,128},{128,96},{160,64},{192,32},{224... | collective-permute-start | bytes 49160 | tf_op jit(solution)/shard_map/ppermute | solution.py:205
  36.8 3.6 %collective-permute-start.5 = (f32[8,512]{1,0:T(8,128)S(1)}, f32[8,512]{1,0:T(8,128)S(1)}, u32[]{:S(2)}, u32[]{:S(2)}) collective-permute-start(f32[8,512]{1,0:T(8,128)S(1)} %add.3.own_ref), channel_id=1, source_target_pairs={{0,96},{32,64},{64,32},{96,0},{128,224},{160,192},{192,160},{224,1... | collective-permute-start | bytes 49160 | tf_op jit(solution)/shard_map/ppermute | solution.py:205
